TPU v7x, 256 devices: a whole 4x4x8 slice. The times are simulated.
256 devices in a mesh: outer: 16 (over z_lo, y), inner: 16 (over x, z_hi, core).
Axes of the slice: x: 4, y: 4, z: 8 (z_hi: 2, z_lo: 4; z = z_hi * 4 + z_lo), core: 2. Of those that a mesh axis runs over, the one named last changes fastest.
Arguments:
- stem_real: float32 [16, 16, 256, 512], P('outer', 'inner'), may hold values from -6 to 6
- stem_imag: float32 [16, 16, 256, 512], P('outer', 'inner'), may hold values from -6 to 6
- branch_real: float32 [4, 512, 512], replicated, may hold values from -0.1875 to 0.1875
- branch_imag: float32 [4, 512, 512], replicated, may hold values from -0.1875 to 0.1875
- orders: int32 [4, 512], replicated, may hold values from 0 to 511, each once within a row
Outputs:
- out_real: float32 [16, 16, 256, 512], P('outer', 'inner')
- out_imag: float32 [16, 16, 256, 512], P('outer', 'inner')
Inputs may be any that keep to these rules, and one draw needn't show every extreme that they name: Each row of orders holds every index of 0 to 511 once.
All inputs are finite; a program needn't handle non-finite values.
Results may differ from a plain program's by a relative error of at most 0.0001.
Values sent between devices are 32-bit elements; how exact they have to be, the bound alone decides.
No kernel may reach another device: no remote copies, remote signals or barrier semaphores. Data moves between devices by JAX's collectives and lax.ppermute only.
A program may use at most 64 MiB of HBM per device.

v0:
```python
import jax
import jax.numpy as jnp
from jax import lax
from jax.sharding import PartitionSpec as P

PRODUCTS = 4


def prepare(branch_real, branch_imag, order):
    width = branch_real.shape[0]
    places = lax.broadcasted_iota(jnp.int32, (width, width), 0)
    selector = (places == order[None, :]).astype(jnp.float32)
    moved_real = jnp.dot(
        selector, branch_real, precision=lax.Precision.HIGHEST, preferred_element_type=jnp.float32
    )
    moved_imag = jnp.dot(
        selector, branch_imag, precision=lax.Precision.HIGHEST, preferred_element_type=jnp.float32
    )
    return (moved_real, moved_imag, moved_real + moved_imag)


def product(plane_real, plane_imag, prepared):
    moved_real, moved_imag, moved_sum = prepared
    width = moved_real.shape[0]
    count = plane_real.size // width
    left_real = plane_real.reshape(count, width)
    left_imag = plane_imag.reshape(count, width)
    first = jnp.dot(
        left_real, moved_real, precision=lax.Precision.HIGHEST, preferred_element_type=jnp.float32
    )
    second = jnp.dot(
        left_imag, moved_imag, precision=lax.Precision.HIGHEST, preferred_element_type=jnp.float32
    )
    third = jnp.dot(
        left_real + left_imag,
        moved_sum,
        precision=lax.Precision.HIGHEST,
        preferred_element_type=jnp.float32,
    )
    return (
        (first - second).reshape(1, 1, count, width),
        (third - first - second).reshape(1, 1, count, width),
    )


def inner_step(plane_real, plane_imag, prepared):
    return product(
        lax.all_to_all(plane_real, "inner", split_axis=3, concat_axis=3, tiled=True),
        lax.all_to_all(plane_imag, "inner", split_axis=3, concat_axis=3, tiled=True),
        prepared,
    )


def outer_step(plane_real, plane_imag, prepared):
    return product(
        lax.all_to_all(plane_real, "outer", split_axis=3, concat_axis=3, tiled=True),
        lax.all_to_all(plane_imag, "outer", split_axis=3, concat_axis=3, tiled=True),
        prepared,
    )


def on_device(stem_real, stem_imag, branch_real, branch_imag, orders):
    tables = [
        prepare(branch_real[step], branch_imag[step], orders[step]) for step in range(PRODUCTS)
    ]
    plane_real, plane_imag = product(stem_real, stem_imag, tables[0])
    plane_real, plane_imag = inner_step(plane_real, plane_imag, tables[1])
    plane_real, plane_imag = outer_step(plane_real, plane_imag, tables[2])
    plane_real, plane_imag = inner_step(plane_real, plane_imag, tables[3])
    return (plane_real, plane_imag)


def solution(mesh):
    placed = (P("outer", "inner", None, None), P("outer", "inner", None, None), P(), P(), P())
    return jax.shard_map(
        on_device,
        mesh=mesh,
        in_specs=placed,
        out_specs=(P("outer", "inner", None, None), P("outer", "inner", None, None)),
        check_vma=False,
    )
```

profile of v0, /device:TPU:33, one launch (start us, length us, event | category | flops | bytes accessed | tf_op | source)
XLA Modules:
  0.0 170.0 jit_solution(8441266659975682407)
XLA Ops:
  1.5 2.3 %fusion.20 = f32[512,512]{1,0:T(8,128)S(1)} fusion(f32[4,512,512]{2,1,0:T(8,128)} %param.8, s32[512]{0:T(512)S(1)} %bitcast.110), kind=kOutput, calls=%fused_computation.26 | convolution fusion | flops 1610874880 | bytes 2099200 | tf_op jit(solution)/shard_map/dot_general | solution.py:16
  3.8 2.3 %fusion.22 = f32[512,512]{1,0:T(8,128)S(1)} fusion(f32[4,512,512]{2,1,0:T(8,128)} %param.7, s32[512]{0:T(512)S(1)} %bitcast.111), kind=kOutput, calls=%fused_computation.28 | convolution fusion | flops 1610874880 | bytes 2099200 | tf_op jit(solution)/shard_map/dot_general | solution.py:13
  13.0 10.7 %all-to-all-start.1 = ((f32[1,1,256,512]{2,1,0,3:T(1,128)}), f32[1,1,256,512]{2,1,0,3:T(1,128)S(1)}, u32[]{:S(2)}, u32[]{:S(2)}) async-start(f32[1,1,256,512]{2,1,0,3:T(1,128)} %copy.10), calls=%async_computation.1 | async-start | bytes 1048576 | tf_op jit(solution)/shard_map/all_to_all | solution.py:49
  25.1 17.8 %all-to-all-done.1 = f32[1,1,256,512]{2,1,0,3:T(1,128)S(1)} async-done(((f32[1,1,256,512]{2,1,0,3:T(1,128)}), f32[1,1,256,512]{2,1,0,3:T(1,128)S(1)}, u32[]{:S(2)}, u32[]{:S(2)}) %all-to-all-start.1) | async-done | bytes 524320 | tf_op jit(solution)/shard_map/all_to_all | solution.py:49
  42.9 5.2 %all-to-all-start = ((f32[1,1,256,512]{2,1,0,3:T(1,128)}), f32[1,1,256,512]{2,1,0,3:T(1,128)}, u32[]{:S(2)}, u32[]{:S(2)}) async-start(f32[1,1,256,512]{2,1,0,3:T(1,128)} %copy.8), calls=%async_computation | async-start | bytes 1048576 | tf_op jit(solution)/shard_map/all_to_all | solution.py:48
  48.1 2.3 %fusion.16 = f32[512,512]{1,0:T(8,128)S(1)} fusion(f32[4,512,512]{2,1,0:T(8,128)} %param.8, s32[512]{0:T(512)S(1)} %bitcast.108), kind=kOutput, calls=%fused_computation.22 | convolution fusion | flops 1610874880 | bytes 2099200 | tf_op jit(solution)/shard_map/dot_general | solution.py:16
  50.4 2.3 %fusion.18 = f32[512,512]{1,0:T(8,128)S(1)} fusion(f32[4,512,512]{2,1,0:T(8,128)} %param.7, s32[512]{0:T(512)S(1)} %bitcast.109), kind=kOutput, calls=%fused_computation.24 | convolution fusion | flops 1610874880 | bytes 2099200 | tf_op jit(solution)/shard_map/dot_general | solution.py:13
  53.8 11.0 %all-to-all-done = f32[1,1,256,512]{2,1,0,3:T(1,128)} async-done(((f32[1,1,256,512]{2,1,0,3:T(1,128)}), f32[1,1,256,512]{2,1,0,3:T(1,128)}, u32[]{:S(2)}, u32[]{:S(2)}) %all-to-all-start) | async-done | bytes 524320 | tf_op jit(solution)/shard_map/all_to_all | solution.py:48
  66.9 3.1 %fusion.3 = f32[1,1,256,512]{3,2,1,0:T(8,128)} fusion(f32[256,512]{1,0:T(8,128)S(1)} %fusion.46, f32[256,512]{1,0:T(8,128)S(1)} %fusion.49, f32[512,512]{1,0:T(8,128)S(1)} %fusion.18, f32[512,512]{1,0:T(8,128)S(1)} %fusion.16, f32[1,1,256,512]{2,1,0,3:T(1,128)} %copy-done.2, f32[1,1,256,512]{2,1,0,3:T(1,128)} %all-to-all-done), kind=kOutput, calls=%fused_computation.7 | convolution fusion | flops 805961728 | bytes 4718592 | tf_op jit(solution)/shard_map/dot_general | solution.py:34
  72.0 5.8 %all-to-all-start.3 = ((f32[1,1,256,512]{2,1,0,3:T(1,128)}), f32[1,1,256,512]{2,1,0,3:T(1,128)S(1)}, u32[]{:S(2)}, u32[]{:S(2)}) async-start(f32[1,1,256,512]{2,1,0,3:T(1,128)} %copy.12), calls=%async_computation.3 | async-start | bytes 1048576 | tf_op jit(solution)/shard_map/all_to_all | solution.py:57
  78.9 12.9 %all-to-all-done.3 = f32[1,1,256,512]{2,1,0,3:T(1,128)S(1)} async-done(((f32[1,1,256,512]{2,1,0,3:T(1,128)}), f32[1,1,256,512]{2,1,0,3:T(1,128)S(1)}, u32[]{:S(2)}, u32[]{:S(2)}) %all-to-all-start.3) | async-done | bytes 524320 | tf_op jit(solution)/shard_map/all_to_all | solution.py:57
  91.8 5.1 %all-to-all-start.2 = ((f32[1,1,256,512]{2,1,0,3:T(1,128)}), f32[1,1,256,512]{2,1,0,3:T(1,128)}, u32[]{:S(2)}, u32[]{:S(2)}) async-start(f32[1,1,256,512]{2,1,0,3:T(1,128)} %copy.11), calls=%async_computation.2 | async-start | bytes 1048576 | tf_op jit(solution)/shard_map/all_to_all | solution.py:56
  96.9 2.4 %fusion.12 = f32[512,512]{1,0:T(8,128)S(1)} fusion(f32[4,512,512]{2,1,0:T(8,128)} %param.8, s32[512]{0:T(512)S(1)} %bitcast.106), kind=kOutput, calls=%fused_computation.18 | convolution fusion | flops 1610874880 | bytes 2099200 | tf_op jit(solution)/shard_map/dot_general | solution.py:16
  99.3 2.3 %fusion.14 = f32[512,512]{1,0:T(8,128)S(1)} fusion(f32[4,512,512]{2,1,0:T(8,128)} %param.7, s32[512]{0:T(512)S(1)} %bitcast.107), kind=kOutput, calls=%fused_computation.20 | convolution fusion | flops 1610874880 | bytes 2099200 | tf_op jit(solution)/shard_map/dot_general | solution.py:13
  102.7 7.9 %all-to-all-done.2 = f32[1,1,256,512]{2,1,0,3:T(1,128)} async-done(((f32[1,1,256,512]{2,1,0,3:T(1,128)}), f32[1,1,256,512]{2,1,0,3:T(1,128)}, u32[]{:S(2)}, u32[]{:S(2)}) %all-to-all-start.2) | async-done | bytes 524320 | tf_op jit(solution)/shard_map/all_to_all | solution.py:56
  110.6 2.1 %fusion.44 = f32[256,512]{1,0:T(8,128)S(1)} fusion(f32[512,512]{1,0:T(8,128)S(1)} %fusion.14, f32[1,1,256,512]{2,1,0,3:T(1,128)} %all-to-all-done.2), kind=kOutput, calls=%fused_computation.56 | convolution fusion | flops 805306368 | bytes 2097152 | tf_op jit(solution)/shard_map/dot_general | solution.py:28
  112.7 3.1 %fusion.5 = f32[1,1,256,512]{3,2,1,0:T(8,128)} fusion(f32[256,512]{1,0:T(8,128)S(1)} %fusion.41, f32[256,512]{1,0:T(8,128)S(1)} %fusion.44, f32[512,512]{1,0:T(8,128)S(1)} %fusion.14, f32[512,512]{1,0:T(8,128)S(1)} %fusion.12, f32[1,1,256,512]{2,1,0,3:T(1,128)} %copy-done.3, f32[1,1,256,512]{2,1,0,3:T(1,128)} %all-to-all-done.2), kind=kOutput, calls=%fused_computation.9 | convolution fusion | flops 805961728 | bytes 4718592 | tf_op jit(solution)/shard_map/dot_general | solution.py:34
  117.8 5.8 %all-to-all-start.5 = ((f32[1,1,256,512]{2,1,0,3:T(1,128)}), f32[1,1,256,512]{2,1,0,3:T(1,128)S(1)}, u32[]{:S(2)}, u32[]{:S(2)}) async-start(f32[1,1,256,512]{2,1,0,3:T(1,128)} %copy.14), calls=%async_computation.5 | async-start | bytes 1048576 | tf_op jit(solution)/shard_map/all_to_all | solution.py:49
  124.7 18.2 %all-to-all-done.5 = f32[1,1,256,512]{2,1,0,3:T(1,128)S(1)} async-done(((f32[1,1,256,512]{2,1,0,3:T(1,128)}), f32[1,1,256,512]{2,1,0,3:T(1,128)S(1)}, u32[]{:S(2)}, u32[]{:S(2)}) %all-to-all-start.5) | async-done | bytes 524320 | tf_op jit(solution)/shard_map/all_to_all | solution.py:49
  142.9 5.2 %all-to-all-start.4 = ((f32[1,1,256,512]{2,1,0,3:T(1,128)}), f32[1,1,256,512]{2,1,0,3:T(1,128)}, u32[]{:S(2)}, u32[]{:S(2)}) async-start(f32[1,1,256,512]{2,1,0,3:T(1,128)} %copy.13), calls=%async_computation.4 | async-start | bytes 1048576 | tf_op jit(solution)/shard_map/all_to_all | solution.py:48
  148.1 2.4 %fusion.8 = f32[512,512]{1,0:T(8,128)S(1)} fusion(f32[4,512,512]{2,1,0:T(8,128)} %param.8, s32[512]{0:T(512)S(1)} %bitcast.104), kind=kOutput, calls=%fused_computation.14 | convolution fusion | flops 1610874880 | bytes 2099200 | tf_op jit(solution)/shard_map/dot_general | solution.py:16
  150.5 2.3 %fusion.10 = f32[512,512]{1,0:T(8,128)S(1)} fusion(f32[4,512,512]{2,1,0:T(8,128)} %param.7, s32[512]{0:T(512)S(1)} %bitcast.105), kind=kOutput, calls=%fused_computation.16 | convolution fusion | flops 1610874880 | bytes 2099200 | tf_op jit(solution)/shard_map/dot_general | solution.py:13
  153.9 10.2 %all-to-all-done.4 = f32[1,1,256,512]{2,1,0,3:T(1,128)} async-done(((f32[1,1,256,512]{2,1,0,3:T(1,128)}), f32[1,1,256,512]{2,1,0,3:T(1,128)}, u32[]{:S(2)}, u32[]{:S(2)}) %all-to-all-start.4) | async-done | bytes 524320 | tf_op jit(solution)/shard_map/all_to_all | solution.py:48
  167.1 3.0 %fusion.7 = f32[1,1,256,512]{3,2,1,0:T(8,128)} fusion(f32[256,512]{1,0:T(8,128)S(1)} %fusion.36, f32[256,512]{1,0:T(8,128)S(1)} %fusion.39, f32[512,512]{1,0:T(8,128)S(1)} %fusion.10, f32[512,512]{1,0:T(8,128)S(1)} %fusion.8, f32[1,1,256,512]{2,1,0,3:T(1,128)S(1)} %copy-done.1, f32[1,1,256,512]{2,1,0,3:T(1,128)} %all-to-all-done.4), kind=kOutput, calls=%fused_computation.11 | convolution fusion | flops 805961728 | bytes 4718592 | tf_op jit(solution)/shard_map/dot_general | solution.py:34
  (33 shorter events, 23.4 us)
Async XLA Ops:
  0.6 5.5 %copy-start.6 = (f32[1,1,256,512]{3,2,1,0:T(8,128)S(1)}, f32[1,1,256,512]{3,2,1,0:T(8,128)}, u32[]{:S(2)}) copy-start(f32[1,1,256,512]{3,2,1,0:T(8,128)} %param.6) | copy-start | bytes 1572868
  0.6 7.3 %copy-start.5 = (f32[1,1,256,512]{3,2,1,0:T(8,128)S(1)}, f32[1,1,256,512]{3,2,1,0:T(8,128)}, u32[]{:S(2)}) copy-start(f32[1,1,256,512]{3,2,1,0:T(8,128)} %param.5) | copy-start | bytes 1572868
  13.0 29.9 %all-to-all-start.1 = ((f32[1,1,256,512]{2,1,0,3:T(1,128)}), f32[1,1,256,512]{2,1,0,3:T(1,128)S(1)}, u32[]{:S(2)}, u32[]{:S(2)}) async-start(f32[1,1,256,512]{2,1,0,3:T(1,128)} %copy.10), calls=%async_computation.1 | async-start | bytes 1048576 | tf_op jit(solution)/shard_map/all_to_all | solution.py:49
  42.9 10.9 %copy-start.2 = (f32[1,1,256,512]{2,1,0,3:T(1,128)}, f32[1,1,256,512]{2,1,0,3:T(1,128)S(1)}, u32[]{:S(2)}) copy-start(f32[1,1,256,512]{2,1,0,3:T(1,128)S(1)} %all-to-all-done.1) | copy-start | bytes 1572868
  42.9 22.0 %all-to-all-start = ((f32[1,1,256,512]{2,1,0,3:T(1,128)}), f32[1,1,256,512]{2,1,0,3:T(1,128)}, u32[]{:S(2)}, u32[]{:S(2)}) async-start(f32[1,1,256,512]{2,1,0,3:T(1,128)} %copy.8), calls=%async_computation | async-start | bytes 1048576 | tf_op jit(solution)/shard_map/all_to_all | solution.py:48
  72.0 19.8 %all-to-all-start.3 = ((f32[1,1,256,512]{2,1,0,3:T(1,128)}), f32[1,1,256,512]{2,1,0,3:T(1,128)S(1)}, u32[]{:S(2)}, u32[]{:S(2)}) async-start(f32[1,1,256,512]{2,1,0,3:T(1,128)} %copy.12), calls=%async_computation.3 | async-start | bytes 1048576 | tf_op jit(solution)/shard_map/all_to_all | solution.py:57
  91.8 5.1 %copy-start.3 = (f32[1,1,256,512]{2,1,0,3:T(1,128)}, f32[1,1,256,512]{2,1,0,3:T(1,128)S(1)}, u32[]{:S(2)}) copy-start(f32[1,1,256,512]{2,1,0,3:T(1,128)S(1)} %all-to-all-done.3) | copy-start | bytes 1572868
  91.8 18.8 %all-to-all-start.2 = ((f32[1,1,256,512]{2,1,0,3:T(1,128)}), f32[1,1,256,512]{2,1,0,3:T(1,128)}, u32[]{:S(2)}, u32[]{:S(2)}) async-start(f32[1,1,256,512]{2,1,0,3:T(1,128)} %copy.11), calls=%async_computation.2 | async-start | bytes 1048576 | tf_op jit(solution)/shard_map/all_to_all | solution.py:56
  96.9 4.7 %copy-start.4 = (f32[1,1,256,512]{2,1,0,3:T(1,128)S(1)}, f32[1,1,256,512]{2,1,0,3:T(1,128)}, u32[]{:S(2)}) copy-start(f32[1,1,256,512]{2,1,0,3:T(1,128)} %copy-done.3) | copy-start | bytes 1572868
  117.8 25.1 %all-to-all-start.5 = ((f32[1,1,256,512]{2,1,0,3:T(1,128)}), f32[1,1,256,512]{2,1,0,3:T(1,128)S(1)}, u32[]{:S(2)}, u32[]{:S(2)}) async-start(f32[1,1,256,512]{2,1,0,3:T(1,128)} %copy.14), calls=%async_computation.5 | async-start | bytes 1048576 | tf_op jit(solution)/shard_map/all_to_all | solution.py:49
  142.9 5.2 %copy-start = (f32[1,1,256,512]{2,1,0,3:T(1,128)}, f32[1,1,256,512]{2,1,0,3:T(1,128)S(1)}, u32[]{:S(2)}) copy-start(f32[1,1,256,512]{2,1,0,3:T(1,128)S(1)} %all-to-all-done.5) | copy-start | bytes 1572868
  142.9 21.2 %all-to-all-start.4 = ((f32[1,1,256,512]{2,1,0,3:T(1,128)}), f32[1,1,256,512]{2,1,0,3:T(1,128)}, u32[]{:S(2)}, u32[]{:S(2)}) async-start(f32[1,1,256,512]{2,1,0,3:T(1,128)} %copy.13), calls=%async_computation.4 | async-start | bytes 1048576 | tf_op jit(solution)/shard_map/all_to_all | solution.py:48
  148.1 4.7 %copy-start.1 = (f32[1,1,256,512]{2,1,0,3:T(1,128)S(1)}, f32[1,1,256,512]{2,1,0,3:T(1,128)}, u32[]{:S(2)}) copy-start(f32[1,1,256,512]{2,1,0,3:T(1,128)} %copy-done) | copy-start | bytes 1572868
where the time goes:
time: 171 us; the launch traced here: 170 us
  waiting for transfers between devices  78 us (46%)
  matrix products  42.7 us (25%)
  starting transfers between devices  37.9 us (22%)
  local copies, waits for them, and re-layouts  9.5 us (6%)
    all_to_all x2, waiting for transfers between devices, inner_step(): lax.all_to_all(plane_imag, 'inner', split_axis=3, concat_axis=3, tiled=True)  36 us
    all_to_all x2, waiting for transfers between devices, inner_step(): lax.all_to_all(plane_real, 'inner', split_axis=3, concat_axis=3, tiled=True)  21.2 us
    all_to_all x2, starting transfers between devices, inner_step(): lax.all_to_all(plane_imag, 'inner', split_axis=3, concat_axis=3, tiled=True)  16.5 us
    all_to_all x1, waiting for transfers between devices, outer_step(): lax.all_to_all(plane_imag, 'outer', split_axis=3, concat_axis=3, tiled=True)  12.9 us
    dot_general x4, matrix products, product(): jnp.dot(left_real + left_imag, moved_sum, precision=lax.Precision.HIGHEST...  11 us
    all_to_all x2, starting transfers between devices, inner_step(): lax.all_to_all(plane_real, 'inner', split_axis=3, concat_axis=3, tiled=True)  10.5 us
    dot_general x4, matrix products, prepare(): jnp.dot(selector, branch_imag, precision=lax.Precision.HIGHEST, preferred...  9.35 us
    dot_general x4, matrix products, prepare(): jnp.dot(selector, branch_real, precision=lax.Precision.HIGHEST, preferred...  9.24 us
  transfers between devices with their start and end apart: 6, of which 6 were waited for; matrix products, arithmetic and copies ran while one was open for 12% of the time, Pallas kernels for 0%

commit v1 on v0

v1 whole, which is shorter than its diff:
```python
import functools

import jax
import jax.numpy as jnp
from jax import lax
from jax.experimental import pallas as pl
from jax.experimental.pallas import tpu as pltpu
from jax.sharding import PartitionSpec as P

PRODUCTS = 4
LANES = 128


def halves(x):
    high = x.astype(jnp.bfloat16)
    return high, (x - high.astype(jnp.float32)).astype(jnp.bfloat16)


def dot(a, b):
    return jnp.dot(a, b, preferred_element_type=jnp.float32)


def tables_kernel(branch_real, branch_imag, orders, tables):
    width = branch_real.shape[1]
    places = lax.broadcasted_iota(jnp.int32, (width, width), 0)
    for p in range(PRODUCTS):
        selector = (places == orders[p, :][None, :]).astype(jnp.float32).astype(jnp.bfloat16)
        moved = []
        for m, plane in enumerate((branch_real, branch_imag)):
            high, low = halves(plane[p])
            high, low = dot(selector, high), dot(selector, low)
            tables[p, 2 * m] = high.astype(jnp.bfloat16)
            tables[p, 2 * m + 1] = low.astype(jnp.bfloat16)
            moved.append(high + low)
        high, low = halves(moved[0] + moved[1])
        tables[p, 4] = high
        tables[p, 5] = low


def pack_kernel(plane_real, plane_imag, packed):
    rows = plane_real.shape[2]
    for m, plane in enumerate((plane_real, plane_imag)):
        for q in range(4):
            packed[pl.ds(4 * m + q, rows, stride=8), :] = plane[0, 0, :, q * LANES:(q + 1) * LANES]


def unpack_kernel(packed, plane_real, plane_imag):
    rows = plane_real.shape[2]
    for m, plane in enumerate((plane_real, plane_imag)):
        for q in range(4):
            plane[0, 0, :, q * LANES:(q + 1) * LANES] = packed[pl.ds(4 * m + q, rows, stride=8), :]


def swap_groups(source, target, major):
    lane = lax.broadcasted_iota(jnp.int32, (16, LANES), 1)
    first_half = lane < 64
    even_group = (lane & 32) == 0
    for m in range(2):
        for q in range(4):
            for g in range(4):
                v = []
                for r in range(4):
                    s = 4 * g + r
                    rows = pl.ds(16 * s, 16) if major else pl.ds(s, 16, stride=16)
                    v.append(source[m, q, rows, :])
                for r in range(2):
                    a, b = v[r], v[r + 2]
                    c = pltpu.roll(jnp.where(first_half, b, a), 64, 1)
                    v[r] = jnp.where(first_half, a, c)
                    v[r + 2] = jnp.where(first_half, c, b)
                for r in (0, 2):
                    a, b = v[r], v[r + 1]
                    v[r] = jnp.where(even_group, a, pltpu.roll(b, 32, 1))
                    v[r + 1] = jnp.where(even_group, pltpu.roll(a, 96, 1), b)
                for t in range(4):
                    target[m, g, pl.ds((4 * q + t) * 16, 16), :] = v[t]


def multiply(real, imag, table):
    real_h, real_l = halves(real)
    imag_h, imag_l = halves(imag)
    sum_h, sum_l = halves(real + imag)
    width = real.shape[1]
    step = 256
    for n in range(width // step):
        columns = pl.ds(n * step, step)
        terms = []
        for k, (high, low) in enumerate(((real_h, real_l), (imag_h, imag_l), (sum_h, sum_l))):
            right_h, right_l = table[2 * k, :, columns], table[2 * k + 1, :, columns]
            terms.append(dot(high, right_h) + dot(high, right_l) + dot(low, right_h))
        out_real, out_imag = terms[0] - terms[1], terms[2] - terms[0] - terms[1]
        for j in range(step // LANES):
            tile = slice(j * LANES, (j + 1) * LANES)
            yield n * (step // LANES) + j, out_real[:, tile], out_imag[:, tile]


def stages_kernel(received, stored, sent, work, turned, tables, arrived):
    rows = received.shape[0] // 8
    fetches = [
        pltpu.make_async_copy(stored.at[p], tables.at[p], arrived.at[p]) for p in range(PRODUCTS)
    ]
    for fetch in fetches:
        fetch.start()

    def joined(m):
        return jnp.concatenate([turned[m, q] for q in range(4)], axis=1)

    for p in range(PRODUCTS):
        if p == 0:
            real, imag = (
                jnp.concatenate([received[pl.ds(4 * m + q, rows, stride=8), :] for q in range(4)], axis=1)
                for m in range(2)
            )
        else:
            swap_groups(work, turned, p == 1)
            real, imag = joined(0), joined(1)
        fetches[p].wait()
        for q, out_real, out_imag in multiply(real, imag, tables.at[p]):
            if p < PRODUCTS - 1:
                work[0, q] = out_real
                work[1, q] = out_imag
            else:
                sent[pl.ds(q, rows, stride=8), :] = out_real
                sent[pl.ds(4 + q, rows, stride=8), :] = out_imag


VMEM = pl.BlockSpec(memory_space=pltpu.VMEM)
HBM = pl.BlockSpec(memory_space=pltpu.HBM)


def call(kernel, out, specs, flops, scratch=(), limit=None):
    return pl.pallas_call(
        kernel,
        out_shape=out,
        in_specs=specs,
        out_specs=jax.tree.map(lambda _: VMEM, out),
        scratch_shapes=scratch,
        compiler_params=pltpu.CompilerParams(vmem_limit_bytes=limit),
        cost_estimate=pl.CostEstimate(flops=flops, bytes_accessed=2**21, transcendentals=0),
    )


def exchange(packed):
    pieces = packed.reshape(-1, 8, LANES)
    pieces = lax.all_to_all(pieces, ("inner", "outer"), split_axis=0, concat_axis=0, tiled=True)
    return pieces.reshape(packed.shape)


def on_device(stem_real, stem_imag, branch_real, branch_imag, orders):
    rows, width = stem_real.shape[2:]
    packed = jax.ShapeDtypeStruct((rows * 8, LANES), jnp.float32)
    plane = jax.ShapeDtypeStruct(stem_real.shape, jnp.float32)
    sent = call(pack_kernel, packed, [VMEM] * 2, 10**6, limit=4 * 2**20)(stem_real, stem_imag)
    tables = call(
        tables_kernel,
        jax.ShapeDtypeStruct((PRODUCTS, 6, width, width), jnp.bfloat16),
        [VMEM] * 3,
        2 * 16 * width**3,
        limit=32 * 2**20,
    )(branch_real, branch_imag, orders)
    received = exchange(sent)
    scratch = [
        pltpu.VMEM((2, 4, rows, LANES), jnp.float32),
        pltpu.VMEM((2, 4, rows, LANES), jnp.float32),
        pltpu.VMEM(tables.shape, tables.dtype),
        pltpu.SemaphoreType.DMA((PRODUCTS,)),
    ]
    flops = 2 * 36 * rows * width**2
    sent = call(stages_kernel, packed, [VMEM, HBM], flops, scratch, 40 * 2**20)(received, tables)
    received = exchange(sent)
    return tuple(call(unpack_kernel, (plane, plane), [VMEM], 10**6, limit=4 * 2**20)(received))


def solution(mesh):
    placed = (P("outer", "inner", None, None), P("outer", "inner", None, None), P(), P(), P())
    return jax.shard_map(
        on_device,
        mesh=mesh,
        in_specs=placed,
        out_specs=(P("outer", "inner", None, None), P("outer", "inner", None, None)),
        check_vma=False,
    )
```

time: 171 us -> 100 us (0.58)
  the two profiles are of different devices: /device:TPU:33 before, /device:TPU:1 now
where the time goes in v1:
time: 100 us; the launch traced here: 99.7 us
  blocking collectives  38 us (38%)
  waiting for transfers between devices  18.1 us (18%)
  Pallas kernels  16.3 us (16%)
  starting transfers between devices  15.6 us (16%)
  local copies, waits for them, and re-layouts  11 us (11%)
    all_to_all x1, blocking collectives, exchange(): lax.all_to_all(pieces, ('inner', 'outer'), split_axis=0, concat_axis=0, t...  38 us
    all_to_all x1, waiting for transfers between devices, exchange(): lax.all_to_all(pieces, ('inner', 'outer'), split_axis=0, concat_axis=0, t...  18.1 us
    all_to_all x1, starting transfers between devices, exchange(): lax.all_to_all(pieces, ('inner', 'outer'), split_axis=0, concat_axis=0, t...  15.6 us
    unnamed x12, local copies, waits for them, and re-layouts  11 us
    pallas_call x1, Pallas kernels, on_device(): call(stages_kernel, packed, [VMEM, HBM], flops, scratch, 40 * 2 ** 20)  8.69 us
    pallas_call x1, Pallas kernels, on_device(): call(tables_kernel, jax.ShapeDtypeStruct((PRODUCTS, 6, width, width), jnp...  5.15 us
  transfers between devices with their start and end apart: 1, of which 1 were waited for; matrix products, arithmetic and copies ran while one was open for 0% of the time, Pallas kernels for 5%

profile of v1, /device:TPU:1, one launch (start us, length us, event | category | flops | bytes accessed | tf_op | source)
XLA Modules:
  0.0 99.7 jit_solution(1213259851065285365)
XLA Ops:
  0.6 0.0 copy-start.3
  0.6 1.0 %copy-done.3 = f32[1,1,256,512]{3,2,1,0:T(8,128)S(1)} copy-done((f32[1,1,256,512]{3,2,1,0:T(8,128)S(1)}, f32[1,1,256,512]{3,2,1,0:T(8,128)}, u32[]{:S(2)}) %copy-start.3) | copy-done | bytes 524312
  1.7 0.0 copy-start.4
  1.7 1.0 %copy-done.4 = f32[1,1,256,512]{3,2,1,0:T(8,128)S(1)} copy-done((f32[1,1,256,512]{3,2,1,0:T(8,128)S(1)}, f32[1,1,256,512]{3,2,1,0:T(8,128)}, u32[]{:S(2)}) %copy-start.4) | copy-done | bytes 524312
  2.7 0.0 copy-start.5
  2.7 1.3 %shard_map.68 = f32[2048,128]{1,0:T(8,128)} custom-call(f32[1,1,256,512]{3,2,1,0:T(8,128)S(1)} %copy-done.3, f32[1,1,256,512]{3,2,1,0:T(8,128)S(1)} %copy-done.4), custom_call_target="tpu_custom_call" | custom-call | flops 1000000 | bytes 2097152 | tf_op jit(solution)/shard_map/pallas_call | solution.py:153
  4.0 15.6 %all-to-all-start = ((f32[256,8,128]{2,1,0:T(8,128)}), f32[256,8,128]{2,1,0:T(8,128)S(1)}, u32[]{:S(2)}, u32[]{:S(2)}) async-start(f32[256,8,128]{2,1,0:T(8,128)} %bitcast), calls=%async_computation | async-start | bytes 2097152 | tf_op jit(solution)/shard_map/all_to_all | solution.py:145
  19.7 0.0 copy-done.5
  19.7 0.0 copy-start.1
  19.7 2.2 %copy-done.1 = f32[4,512,512]{2,1,0:T(8,128)S(1)} copy-done((f32[4,512,512]{2,1,0:T(8,128)S(1)}, f32[4,512,512]{2,1,0:T(8,128)}, u32[]{:S(2)}) %copy-start.1) | copy-done | bytes 4194328
  21.9 0.0 copy-start.2
  21.9 2.2 %copy-done.2 = f32[4,512,512]{2,1,0:T(8,128)S(1)} copy-done((f32[4,512,512]{2,1,0:T(8,128)S(1)}, f32[4,512,512]{2,1,0:T(8,128)}, u32[]{:S(2)}) %copy-start.2) | copy-done | bytes 4194328
  24.1 5.1 %shard_map.69.stored = bf16[4,6,512,512]{3,2,1,0:T(8,128)(2,1)S(1)} custom-call(f32[4,512,512]{2,1,0:T(8,128)S(1)} %copy-done.1, f32[4,512,512]{2,1,0:T(8,128)S(1)} %copy-done.2, s32[4,512]{1,0:T(4,128)S(1)} %copy-done.5), custom_call_target="tpu_custom_call" | custom-call | flops 4294967296 | bytes 2097152 | tf_op jit(solution)/shard_map/pallas_call | solution.py:154
  29.2 0.0 copy-start
  29.2 4.5 %copy-done = bf16[4,6,512,512]{3,2,1,0:T(8,128)(2,1)} copy-done((bf16[4,6,512,512]{3,2,1,0:T(8,128)(2,1)}, bf16[4,6,512,512]{3,2,1,0:T(8,128)(2,1)S(1)}, u32[]{:S(2)}) %copy-start) | copy-done | bytes 12582936
  33.7 18.1 %all-to-all-done = f32[256,8,128]{2,1,0:T(8,128)S(1)} async-done(((f32[256,8,128]{2,1,0:T(8,128)}), f32[256,8,128]{2,1,0:T(8,128)S(1)}, u32[]{:S(2)}, u32[]{:S(2)}) %all-to-all-start) | async-done | bytes 1048608 | tf_op jit(solution)/shard_map/all_to_all | solution.py:145
  51.8 8.7 %shard_map.70 = f32[2048,128]{1,0:T(8,128)S(1)} custom-call(f32[2048,128]{1,0:T(8,128)S(1)} %bitcast.5, bf16[4,6,512,512]{3,2,1,0:T(8,128)(2,1)} %copy-done), custom_call_target="tpu_custom_call" | custom-call | flops 4831838208 | bytes 2097152 | tf_op jit(solution)/shard_map/pallas_call | solution.py:169
  60.5 38.0 %all_to_all.10 = f32[256,8,128]{2,1,0:T(8,128)S(1)} all-to-all(f32[256,8,128]{2,1,0:T(8,128)S(1)} %bitcast.6), channel_id=1, replica_groups=mesh['outer'=16,'inner'=16] {'inner','outer'}, dimensions={0} | all-to-all | bytes 2097152 | tf_op jit(solution)/shard_map/all_to_all | solution.py:145
  98.5 1.2 %shard_map.71 = (f32[1,1,256,512]{3,2,1,0:T(8,128)}, f32[1,1,256,512]{3,2,1,0:T(8,128)}) custom-call(f32[2048,128]{1,0:T(8,128)S(1)} %bitcast.4), custom_call_target="tpu_custom_call" | custom-call | flops 1000000 | bytes 2097152 | tf_op jit(solution)/shard_map/pallas_call | solution.py:171
Async XLA Ops:
  0.6 1.0 %copy-start.3 = (f32[1,1,256,512]{3,2,1,0:T(8,128)S(1)}, f32[1,1,256,512]{3,2,1,0:T(8,128)}, u32[]{:S(2)}) copy-start(f32[1,1,256,512]{3,2,1,0:T(8,128)} %plane_real.1) | copy-start | bytes 1572868
  1.7 1.0 %copy-start.4 = (f32[1,1,256,512]{3,2,1,0:T(8,128)S(1)}, f32[1,1,256,512]{3,2,1,0:T(8,128)}, u32[]{:S(2)}) copy-start(f32[1,1,256,512]{3,2,1,0:T(8,128)} %plane_imag.1) | copy-start | bytes 1572868
  2.7 16.9 %copy-start.5 = (s32[4,512]{1,0:T(4,128)S(1)}, s32[4,512]{1,0:T(4,128)}, u32[]{:S(2)}) copy-start(s32[4,512]{1,0:T(4,128)} %orders.1) | copy-start | bytes 24580
  4.0 47.8 %all-to-all-start = ((f32[256,8,128]{2,1,0:T(8,128)}), f32[256,8,128]{2,1,0:T(8,128)S(1)}, u32[]{:S(2)}, u32[]{:S(2)}) async-start(f32[256,8,128]{2,1,0:T(8,128)} %bitcast), calls=%async_computation | async-start | bytes 2097152 | tf_op jit(solution)/shard_map/all_to_all | solution.py:145
  19.7 2.2 %copy-start.1 = (f32[4,512,512]{2,1,0:T(8,128)S(1)}, f32[4,512,512]{2,1,0:T(8,128)}, u32[]{:S(2)}) copy-start(f32[4,512,512]{2,1,0:T(8,128)} %branch_real.1) | copy-start | bytes 12582916
  21.9 2.2 %copy-start.2 = (f32[4,512,512]{2,1,0:T(8,128)S(1)}, f32[4,512,512]{2,1,0:T(8,128)}, u32[]{:S(2)}) copy-start(f32[4,512,512]{2,1,0:T(8,128)} %branch_imag.1) | copy-start | bytes 12582916
  29.2 4.5 %copy-start = (bf16[4,6,512,512]{3,2,1,0:T(8,128)(2,1)}, bf16[4,6,512,512]{3,2,1,0:T(8,128)(2,1)S(1)}, u32[]{:S(2)}) copy-start(bf16[4,6,512,512]{3,2,1,0:T(8,128)(2,1)S(1)} %shard_map.69.stored) | copy-start | bytes 37748740

commit v2 on v1

--- a/solution.py
+++ b/solution.py
@@ -9,6 +9,7 @@
 
 PRODUCTS = 4
 LANES = 128
+PARTS = 4
 
 
 def halves(x):
@@ -37,18 +38,53 @@
         tables[p, 5] = low
 
 
-def pack_kernel(plane_real, plane_imag, packed):
+def pack_kernel(plane_real, plane_imag, packed, planes, tiles, arrived, left):
     rows = plane_real.shape[2]
-    for m, plane in enumerate((plane_real, plane_imag)):
-        for q in range(4):
-            packed[pl.ds(4 * m + q, rows, stride=8), :] = plane[0, 0, :, q * LANES:(q + 1) * LANES]
-
-
-def unpack_kernel(packed, plane_real, plane_imag):
+    part = rows // PARTS
+    sources = (plane_real, plane_imag)
+    fetches = [
+        [
+            pltpu.make_async_copy(
+                source.at[0, 0, pl.ds(c * part, part)], planes.at[m, pl.ds(c * part, part)], arrived.at[m, c]
+            )
+            for m, source in enumerate(sources)
+        ]
+        for c in range(PARTS)
+    ]
+    for pair in fetches:
+        for fetch in pair:
+            fetch.start()
+    leaves = []
+    for c, pair in enumerate(fetches):
+        for m, fetch in enumerate(pair):
+            fetch.wait()
+            for q in range(4):
+                value = planes[m, pl.ds(c * part, part), q * LANES:(q + 1) * LANES]
+                tiles[pl.ds(8 * c * part + 4 * m + q, part, stride=8), :] = value
+        lines = pl.ds(8 * c * part, 8 * part)
+        leaves.append(pltpu.make_async_copy(tiles.at[lines], packed.at[lines], left.at[c]))
+        leaves[-1].start()
+    for leave in leaves:
+        leave.wait()
+
+
+def unpack_kernel(packed, plane_real, plane_imag, planes, left):
     rows = plane_real.shape[2]
-    for m, plane in enumerate((plane_real, plane_imag)):
-        for q in range(4):
-            plane[0, 0, :, q * LANES:(q + 1) * LANES] = packed[pl.ds(4 * m + q, rows, stride=8), :]
+    part = rows // PARTS
+    leaves = []
+    for c in range(PARTS):
+        for m, target in enumerate((plane_real, plane_imag)):
+            for q in range(4):
+                value = packed[pl.ds(8 * c * part + 4 * m + q, part, stride=8), :]
+                planes[m, pl.ds(c * part, part), q * LANES:(q + 1) * LANES] = value
+            leaves.append(
+                pltpu.make_async_copy(
+                    planes.at[m, pl.ds(c * part, part)], target.at[0, 0, pl.ds(c * part, part)], left.at[m, c]
+                )
+            )
+            leaves[-1].start()
+    for leave in leaves:
+        leave.wait()
 
 
 def swap_groups(source, target, major):
@@ -61,7 +97,7 @@
                 v = []
                 for r in range(4):
                     s = 4 * g + r
-                    rows = pl.ds(16 * s, 16) if major else pl.ds(s, 16, stride=16)
+                    rows = pl.ds(24 * s, 16) if major else pl.ds(s, 16, stride=24)
                     v.append(source[m, q, rows, :])
                 for r in range(2):
                     a, b = v[r], v[r + 2]
@@ -76,25 +112,24 @@
                     target[m, g, pl.ds((4 * q + t) * 16, 16), :] = v[t]
 
 
-def multiply(real, imag, table):
-    real_h, real_l = halves(real)
-    imag_h, imag_l = halves(imag)
-    sum_h, sum_l = halves(real + imag)
+def multiply(real, imag, table, left):
+    for k, plane in enumerate((real, imag, real + imag)):
+        left[2 * k], left[2 * k + 1] = halves(plane)
     width = real.shape[1]
     step = 256
     for n in range(width // step):
         columns = pl.ds(n * step, step)
         terms = []
-        for k, (high, low) in enumerate(((real_h, real_l), (imag_h, imag_l), (sum_h, sum_l))):
+        for k, (high, low) in enumerate(((left[0], left[1]), (left[2], left[3]), (left[4], left[5]))):
             right_h, right_l = table[2 * k, :, columns], table[2 * k + 1, :, columns]
-            terms.append(dot(high, right_h) + dot(high, right_l) + dot(low, right_h))
+            terms.append(dot(high, right_h) + dot(low, right_h) + dot(high, right_l))
         out_real, out_imag = terms[0] - terms[1], terms[2] - terms[0] - terms[1]
         for j in range(step // LANES):
             tile = slice(j * LANES, (j + 1) * LANES)
             yield n * (step // LANES) + j, out_real[:, tile], out_imag[:, tile]
 
 
-def stages_kernel(received, stored, sent, work, turned, tables, arrived):
+def stages_kernel(received, stored, sent, work, turned, tables, left, arrived):
     rows = received.shape[0] // 8
     fetches = [
         pltpu.make_async_copy(stored.at[p], tables.at[p], arrived.at[p]) for p in range(PRODUCTS)
@@ -115,10 +150,11 @@
             swap_groups(work, turned, p == 1)
             real, imag = joined(0), joined(1)
         fetches[p].wait()
-        for q, out_real, out_imag in multiply(real, imag, tables.at[p]):
+        for q, out_real, out_imag in multiply(real, imag, tables.at[p], left):
             if p < PRODUCTS - 1:
-                work[0, q] = out_real
-                work[1, q] = out_imag
+                for u in range(16):
+                    work[0, q, 24 * u:24 * u + 16] = out_real[16 * u:16 * u + 16]
+                    work[1, q, 24 * u:24 * u + 16] = out_imag[16 * u:16 * u + 16]
             else:
                 sent[pl.ds(q, rows, stride=8), :] = out_real
                 sent[pl.ds(4 + q, rows, stride=8), :] = out_imag
@@ -128,12 +164,12 @@
 HBM = pl.BlockSpec(memory_space=pltpu.HBM)
 
 
-def call(kernel, out, specs, flops, scratch=(), limit=None):
+def call(kernel, out, ins, outs, flops, scratch=(), limit=None):
     return pl.pallas_call(
         kernel,
         out_shape=out,
-        in_specs=specs,
-        out_specs=jax.tree.map(lambda _: VMEM, out),
+        in_specs=ins,
+        out_specs=outs,
         scratch_shapes=scratch,
         compiler_params=pltpu.CompilerParams(vmem_limit_bytes=limit),
         cost_estimate=pl.CostEstimate(flops=flops, bytes_accessed=2**21, transcendentals=0),
@@ -150,25 +186,30 @@
     rows, width = stem_real.shape[2:]
     packed = jax.ShapeDtypeStruct((rows * 8, LANES), jnp.float32)
     plane = jax.ShapeDtypeStruct(stem_real.shape, jnp.float32)
-    sent = call(pack_kernel, packed, [VMEM] * 2, 10**6, limit=4 * 2**20)(stem_real, stem_imag)
-    tables = call(
-        tables_kernel,
-        jax.ShapeDtypeStruct((PRODUCTS, 6, width, width), jnp.bfloat16),
-        [VMEM] * 3,
-        2 * 16 * width**3,
-        limit=32 * 2**20,
-    )(branch_real, branch_imag, orders)
+    planes = pltpu.VMEM((2, rows, width), jnp.float32)
+    tiled = pltpu.VMEM((2, 4, rows, LANES), jnp.float32)
+    dma = pltpu.SemaphoreType.DMA
+    scratch = [planes, pltpu.VMEM(packed.shape, packed.dtype), dma((2, PARTS)), dma((PARTS,))]
+    sent = call(pack_kernel, packed, [HBM] * 2, HBM, 10**6, scratch)(stem_real, stem_imag)
+    stored = jax.ShapeDtypeStruct((PRODUCTS, 6, width, width), jnp.bfloat16)
+    stored = call(tables_kernel, stored, [VMEM] * 3, VMEM, 32 * width**3, (), 32 * 2**20)(
+        branch_real, branch_imag, orders
+    )
     received = exchange(sent)
     scratch = [
-        pltpu.VMEM((2, 4, rows, LANES), jnp.float32),
-        pltpu.VMEM((2, 4, rows, LANES), jnp.float32),
-        pltpu.VMEM(tables.shape, tables.dtype),
-        pltpu.SemaphoreType.DMA((PRODUCTS,)),
+        pltpu.VMEM((2, 4, 384, LANES), jnp.float32),
+        tiled,
+        pltpu.VMEM(stored.shape, stored.dtype),
+        pltpu.VMEM((6, rows, width), stored.dtype),
+        dma((PRODUCTS,)),
     ]
     flops = 2 * 36 * rows * width**2
-    sent = call(stages_kernel, packed, [VMEM, HBM], flops, scratch, 40 * 2**20)(received, tables)
+    sent = call(stages_kernel, packed, [VMEM, HBM], VMEM, flops, scratch, 40 * 2**20)(received, stored)
     received = exchange(sent)
-    return tuple(call(unpack_kernel, (plane, plane), [VMEM], 10**6, limit=4 * 2**20)(received))
+    scratch = [planes, dma((2, PARTS))]
+    return tuple(
+        call(unpack_kernel, (plane, plane), [VMEM], (HBM, HBM), 10**6, scratch, 4 * 2**20)(received)
+    )
 
 
 def solution(mesh):

time: 100 us -> 98.5 us (0.985)
  local copies, waits for them, and re-layouts: 11 us -> 8.91 us
    unnamed x12 -> x8, local copies, waits for them, and re-layouts: 11 us -> 8.91 us
where the time goes in v2:
time: 98.5 us; the launch traced here: 98.2 us
  blocking collectives  38 us (39%)
  waiting for transfers between devices  18.1 us (18%)
  Pallas kernels  16.9 us (17%)
  starting transfers between devices  15.7 us (16%)
  local copies, waits for them, and re-layouts  8.91 us (9%)
    all_to_all x1, blocking collectives, exchange(): lax.all_to_all(pieces, ('inner', 'outer'), split_axis=0, concat_axis=0, t...  38 us
    all_to_all x1, waiting for transfers between devices, exchange(): lax.all_to_all(pieces, ('inner', 'outer'), split_axis=0, concat_axis=0, t...  18.1 us
    all_to_all x1, starting transfers between devices, exchange(): lax.all_to_all(pieces, ('inner', 'outer'), split_axis=0, concat_axis=0, t...  15.7 us
    unnamed x8, local copies, waits for them, and re-layouts  8.91 us
    pallas_call x1, Pallas kernels, on_device(): call(stages_kernel, packed, [VMEM, HBM], VMEM, flops, scratch, 40 * 2 ** 20)  8.49 us
    pallas_call x1, Pallas kernels, on_device(): call(tables_kernel, stored, [VMEM] * 3, VMEM, 32 * width ** 3, (), 32 * 2...  5.14 us
    pallas_call x1, Pallas kernels, on_device(): call(pack_kernel, packed, [HBM] * 2, HBM, 10 ** 6, scratch)  2.17 us
  transfers between devices with their start and end apart: 1, of which 1 were waited for; matrix products, arithmetic and copies ran while one was open for 0% of the time, Pallas kernels for 5%

profile of v2, /device:TPU:1, one launch (start us, length us, event | category | flops | bytes accessed | tf_op | source)
XLA Modules:
  0.0 98.2 jit_solution(13739277947644271852)
XLA Ops:
  0.6 0.0 copy-start.3
  0.6 2.2 %shard_map.68 = f32[2048,128]{1,0:T(8,128)} custom-call(f32[1,1,256,512]{3,2,1,0:T(8,128)} %plane_real.1, f32[1,1,256,512]{3,2,1,0:T(8,128)} %plane_imag.1), custom_call_target="tpu_custom_call" | custom-call | flops 1000000 | bytes 2097152 | tf_op jit(solution)/shard_map/pallas_call | solution.py:193
  2.8 15.7 %all-to-all-start = ((f32[256,8,128]{2,1,0:T(8,128)}), f32[256,8,128]{2,1,0:T(8,128)S(1)}, u32[]{:S(2)}, u32[]{:S(2)}) async-start(f32[256,8,128]{2,1,0:T(8,128)} %bitcast.7), calls=%async_computation | async-start | bytes 2097152 | tf_op jit(solution)/shard_map/all_to_all | solution.py:181
  18.5 0.0 copy-done.3
  18.5 0.0 copy-start.1
  18.5 2.2 %copy-done.1 = f32[4,512,512]{2,1,0:T(8,128)S(1)} copy-done((f32[4,512,512]{2,1,0:T(8,128)S(1)}, f32[4,512,512]{2,1,0:T(8,128)}, u32[]{:S(2)}) %copy-start.1) | copy-done | bytes 4194328
  20.7 0.0 copy-start.2
  20.7 2.2 %copy-done.2 = f32[4,512,512]{2,1,0:T(8,128)S(1)} copy-done((f32[4,512,512]{2,1,0:T(8,128)S(1)}, f32[4,512,512]{2,1,0:T(8,128)}, u32[]{:S(2)}) %copy-start.2) | copy-done | bytes 4194328
  22.9 5.1 %shard_map.69.stored = bf16[4,6,512,512]{3,2,1,0:T(8,128)(2,1)S(1)} custom-call(f32[4,512,512]{2,1,0:T(8,128)S(1)} %copy-done.1, f32[4,512,512]{2,1,0:T(8,128)S(1)} %copy-done.2, s32[4,512]{1,0:T(4,128)S(1)} %copy-done.3), custom_call_target="tpu_custom_call" | custom-call | flops 4294967296 | bytes 2097152 | tf_op jit(solution)/shard_map/pallas_call | solution.py:195
  28.0 0.0 copy-start
  28.0 4.5 %copy-done = bf16[4,6,512,512]{3,2,1,0:T(8,128)(2,1)} copy-done((bf16[4,6,512,512]{3,2,1,0:T(8,128)(2,1)}, bf16[4,6,512,512]{3,2,1,0:T(8,128)(2,1)S(1)}, u32[]{:S(2)}) %copy-start) | copy-done | bytes 12582936
  32.6 18.1 %all-to-all-done = f32[256,8,128]{2,1,0:T(8,128)S(1)} async-done(((f32[256,8,128]{2,1,0:T(8,128)}), f32[256,8,128]{2,1,0:T(8,128)S(1)}, u32[]{:S(2)}, u32[]{:S(2)}) %all-to-all-start) | async-done | bytes 1048608 | tf_op jit(solution)/shard_map/all_to_all | solution.py:181
  50.6 8.5 %shard_map.70 = f32[2048,128]{1,0:T(8,128)S(1)} custom-call(f32[2048,128]{1,0:T(8,128)S(1)} %bitcast.5, bf16[4,6,512,512]{3,2,1,0:T(8,128)(2,1)} %copy-done), custom_call_target="tpu_custom_call" | custom-call | flops 4831838208 | bytes 2097152 | tf_op jit(solution)/shard_map/pallas_call | solution.py:207
  59.1 38.0 %all_to_all.10 = f32[256,8,128]{2,1,0:T(8,128)S(1)} all-to-all(f32[256,8,128]{2,1,0:T(8,128)S(1)} %bitcast.6), channel_id=1, replica_groups=mesh['outer'=16,'inner'=16] {'inner','outer'}, dimensions={0} | all-to-all | bytes 2097152 | tf_op jit(solution)/shard_map/all_to_all | solution.py:181
  97.2 1.0 %shard_map.71 = (f32[1,1,256,512]{3,2,1,0:T(8,128)}, f32[1,1,256,512]{3,2,1,0:T(8,128)}) custom-call(f32[2048,128]{1,0:T(8,128)S(1)} %bitcast.4), custom_call_target="tpu_custom_call" | custom-call | flops 1000000 | bytes 2097152 | tf_op jit(solution)/shard_map/pallas_call | solution.py:211
Async XLA Ops:
  0.6 17.9 %copy-start.3 = (s32[4,512]{1,0:T(4,128)S(1)}, s32[4,512]{1,0:T(4,128)}, u32[]{:S(2)}) copy-start(s32[4,512]{1,0:T(4,128)} %orders.1) | copy-start | bytes 24580
  2.8 47.8 %all-to-all-start = ((f32[256,8,128]{2,1,0:T(8,128)}), f32[256,8,128]{2,1,0:T(8,128)S(1)}, u32[]{:S(2)}, u32[]{:S(2)}) async-start(f32[256,8,128]{2,1,0:T(8,128)} %bitcast.7), calls=%async_computation | async-start | bytes 2097152 | tf_op jit(solution)/shard_map/all_to_all | solution.py:181
  18.5 2.2 %copy-start.1 = (f32[4,512,512]{2,1,0:T(8,128)S(1)}, f32[4,512,512]{2,1,0:T(8,128)}, u32[]{:S(2)}) copy-start(f32[4,512,512]{2,1,0:T(8,128)} %branch_real.1) | copy-start | bytes 12582916
  20.7 2.2 %copy-start.2 = (f32[4,512,512]{2,1,0:T(8,128)S(1)}, f32[4,512,512]{2,1,0:T(8,128)}, u32[]{:S(2)}) copy-start(f32[4,512,512]{2,1,0:T(8,128)} %branch_imag.1) | copy-start | bytes 12582916
  28.0 4.5 %copy-start = (bf16[4,6,512,512]{3,2,1,0:T(8,128)(2,1)}, bf16[4,6,512,512]{3,2,1,0:T(8,128)(2,1)S(1)}, u32[]{:S(2)}) copy-start(bf16[4,6,512,512]{3,2,1,0:T(8,128)(2,1)S(1)} %shard_map.69.stored) | copy-start | bytes 37748740

commit v3 on v2

--- a/solution.py
+++ b/solution.py
@@ -21,21 +21,28 @@
     return jnp.dot(a, b, preferred_element_type=jnp.float32)
 
 
-def tables_kernel(branch_real, branch_imag, orders, tables):
+def spans():
+    counts = [2] + [6] * (PRODUCTS - 1)
+    return [pl.ds(sum(counts[:p]), count) for p, count in enumerate(counts)]
+
+
+def tables_kernel(branch_real, branch_imag, orders, first, stored):
     width = branch_real.shape[1]
     places = lax.broadcasted_iota(jnp.int32, (width, width), 0)
-    for p in range(PRODUCTS):
+    for p, span in enumerate(spans()):
         selector = (places == orders[p, :][None, :]).astype(jnp.float32).astype(jnp.bfloat16)
+        last = span.start + span.size
         moved = []
         for m, plane in enumerate((branch_real, branch_imag)):
             high, low = halves(plane[p])
             high, low = dot(selector, high), dot(selector, low)
-            tables[p, 2 * m] = high.astype(jnp.bfloat16)
-            tables[p, 2 * m + 1] = low.astype(jnp.bfloat16)
+            table, place = (first, 2 * m) if p == 0 else (stored, span.start + 2 * m)
+            table[place] = high.astype(jnp.bfloat16)
+            table[place + 1] = low.astype(jnp.bfloat16)
             moved.append(high + low)
         high, low = halves(moved[0] + moved[1])
-        tables[p, 4] = high
-        tables[p, 5] = low
+        stored[last - 2] = high
+        stored[last - 1] = low
 
 
 def pack_kernel(plane_real, plane_imag, packed, planes, tiles, arrived, left):
@@ -112,16 +119,19 @@
                     target[m, g, pl.ds((4 * q + t) * 16, 16), :] = v[t]
 
 
-def multiply(real, imag, table, left):
+def multiply(real, imag, tables, left, ready):
     for k, plane in enumerate((real, imag, real + imag)):
         left[2 * k], left[2 * k + 1] = halves(plane)
     width = real.shape[1]
     step = 256
     for n in range(width // step):
-        columns = pl.ds(n * step, step)
+        columns = slice(n * step, (n + 1) * step)
         terms = []
-        for k, (high, low) in enumerate(((left[0], left[1]), (left[2], left[3]), (left[4], left[5]))):
-            right_h, right_l = table[2 * k, :, columns], table[2 * k + 1, :, columns]
+        for k in range(3):
+            if n == 0:
+                ready(k)
+            high, low = left[2 * k], left[2 * k + 1]
+            right_h, right_l = (table[place, :, columns] for table, place in tables[2 * k:2 * k + 2])
             terms.append(dot(high, right_h) + dot(low, right_h) + dot(high, right_l))
         out_real, out_imag = terms[0] - terms[1], terms[2] - terms[0] - terms[1]
         for j in range(step // LANES):
@@ -129,18 +139,15 @@
             yield n * (step // LANES) + j, out_real[:, tile], out_imag[:, tile]
 
 
-def stages_kernel(received, stored, sent, work, turned, tables, left, arrived):
+def stages_kernel(received, first, stored, sent, work, turned, later, left, arrived):
     rows = received.shape[0] // 8
     fetches = [
-        pltpu.make_async_copy(stored.at[p], tables.at[p], arrived.at[p]) for p in range(PRODUCTS)
+        pltpu.make_async_copy(stored.at[span], later.at[span], arrived.at[p]) for p, span in enumerate(spans())
     ]
-    for fetch in fetches:
-        fetch.start()
-
-    def joined(m):
-        return jnp.concatenate([turned[m, q] for q in range(4)], axis=1)
-
-    for p in range(PRODUCTS):
+    for p, fetch in enumerate(fetches):
+        fetch.start(priority=min(p, 1))
+
+    for p, span in enumerate(spans()):
         if p == 0:
             real, imag = (
                 jnp.concatenate([received[pl.ds(4 * m + q, rows, stride=8), :] for q in range(4)], axis=1)
@@ -148,9 +155,16 @@
             )
         else:
             swap_groups(work, turned, p == 1)
-            real, imag = joined(0), joined(1)
-        fetches[p].wait()
-        for q, out_real, out_imag in multiply(real, imag, tables.at[p], left):
+            real, imag = (jnp.concatenate([turned[m, q] for q in range(4)], axis=1) for m in range(2))
+        tables = [(later, span.start + j) for j in range(span.size)]
+        if p == 0:
+            tables = [(first, j) for j in range(4)] + tables
+
+        def ready(k, p=p):
+            if k == (2 if p == 0 else 0):
+                fetches[p].wait()
+
+        for q, out_real, out_imag in multiply(real, imag, tables, left, ready):
             if p < PRODUCTS - 1:
                 for u in range(16):
                     work[0, q, 24 * u:24 * u + 16] = out_real[16 * u:16 * u + 16]
@@ -191,10 +205,11 @@
     dma = pltpu.SemaphoreType.DMA
     scratch = [planes, pltpu.VMEM(packed.shape, packed.dtype), dma((2, PARTS)), dma((PARTS,))]
     sent = call(pack_kernel, packed, [HBM] * 2, HBM, 10**6, scratch)(stem_real, stem_imag)
-    stored = jax.ShapeDtypeStruct((PRODUCTS, 6, width, width), jnp.bfloat16)
-    stored = call(tables_kernel, stored, [VMEM] * 3, VMEM, 32 * width**3, (), 32 * 2**20)(
-        branch_real, branch_imag, orders
-    )
+    first = jax.ShapeDtypeStruct((4, width, width), jnp.bfloat16)
+    stored = jax.ShapeDtypeStruct((6 * PRODUCTS - 4, width, width), jnp.bfloat16)
+    first, stored = call(
+        tables_kernel, (first, stored), [VMEM] * 3, (VMEM, VMEM), 32 * width**3, (), 32 * 2**20
+    )(branch_real, branch_imag, orders)
     received = exchange(sent)
     scratch = [
         pltpu.VMEM((2, 4, 384, LANES), jnp.float32),
@@ -204,7 +219,9 @@
         dma((PRODUCTS,)),
     ]
     flops = 2 * 36 * rows * width**2
-    sent = call(stages_kernel, packed, [VMEM, HBM], VMEM, flops, scratch, 40 * 2**20)(received, stored)
+    sent = call(stages_kernel, packed, [VMEM, VMEM, HBM], VMEM, flops, scratch, 40 * 2**20)(
+        received, first, stored
+    )
     received = exchange(sent)
     scratch = [planes, dma((2, PARTS))]
     return tuple(

time: 98.5 us -> 97.3 us (0.988)
  Pallas kernels: 16.9 us -> 15.7 us
    pallas_call x2, Pallas kernels: 13.6 us -> 12.5 us  [the longest x1 7.38 us: on_device(): call(stages_kernel, packed, [VMEM, VMEM, HBM], VMEM, flops, scratch, 40 *...]
where the time goes in v3:
time: 97.3 us; the launch traced here: 97.1 us
  blocking collectives  38 us (39%)
  waiting for transfers between devices  18.6 us (19%)
  Pallas kernels  15.7 us (16%)
  starting transfers between devices  15.7 us (16%)
  local copies, waits for them, and re-layouts  8.34 us (9%)
    all_to_all x1, blocking collectives, exchange(): lax.all_to_all(pieces, ('inner', 'outer'), split_axis=0, concat_axis=0, t...  38 us
    all_to_all x1, waiting for transfers between devices, exchange(): lax.all_to_all(pieces, ('inner', 'outer'), split_axis=0, concat_axis=0, t...  18.6 us
    all_to_all x1, starting transfers between devices, exchange(): lax.all_to_all(pieces, ('inner', 'outer'), split_axis=0, concat_axis=0, t...  15.7 us
    unnamed x8, local copies, waits for them, and re-layouts  8.34 us
    pallas_call x1, Pallas kernels, on_device(): call(stages_kernel, packed, [VMEM, VMEM, HBM], VMEM, flops, scratch, 40 *...  7.38 us
    pallas_call x1, Pallas kernels, on_device(): call(tables_kernel, (first, stored), [VMEM] * 3, (VMEM, VMEM), 32 * width...  5.14 us
    pallas_call x1, Pallas kernels, on_device(): call(pack_kernel, packed, [HBM] * 2, HBM, 10 ** 6, scratch)  2.13 us
  transfers between devices with their start and end apart: 1, of which 1 were waited for; matrix products, arithmetic and copies ran while one was open for 0% of the time, Pallas kernels for 5%

profile of v3, /device:TPU:1, one launch (start us, length us, event | category | flops | bytes accessed | tf_op | source)
XLA Modules:
  0.0 97.1 jit_solution(15706141271620677518)
XLA Ops:
  0.6 0.0 copy-start.2
  0.6 2.1 %shard_map.68 = f32[2048,128]{1,0:T(8,128)} custom-call(f32[1,1,256,512]{3,2,1,0:T(8,128)} %plane_real.1, f32[1,1,256,512]{3,2,1,0:T(8,128)} %plane_imag.1), custom_call_target="tpu_custom_call" | custom-call | flops 1000000 | bytes 2097152 | tf_op jit(solution)/shard_map/pallas_call | solution.py:207
  2.8 15.7 %all-to-all-start = ((f32[256,8,128]{2,1,0:T(8,128)}), f32[256,8,128]{2,1,0:T(8,128)S(1)}, u32[]{:S(2)}, u32[]{:S(2)}) async-start(f32[256,8,128]{2,1,0:T(8,128)} %bitcast.7), calls=%async_computation | async-start | bytes 2097152 | tf_op jit(solution)/shard_map/all_to_all | solution.py:195
  18.4 0.0 copy-done.2
  18.5 0.0 copy-start
  18.5 2.2 %copy-done = f32[4,512,512]{2,1,0:T(8,128)S(1)} copy-done((f32[4,512,512]{2,1,0:T(8,128)S(1)}, f32[4,512,512]{2,1,0:T(8,128)}, u32[]{:S(2)}) %copy-start) | copy-done | bytes 4194328
  20.6 0.0 copy-start.1
  20.6 2.2 %copy-done.1 = f32[4,512,512]{2,1,0:T(8,128)S(1)} copy-done((f32[4,512,512]{2,1,0:T(8,128)S(1)}, f32[4,512,512]{2,1,0:T(8,128)}, u32[]{:S(2)}) %copy-start.1) | copy-done | bytes 4194328
  22.8 5.1 %shard_map.69 = (bf16[4,512,512]{2,1,0:T(8,128)(2,1)S(1)}, bf16[20,512,512]{2,1,0:T(8,128)(2,1)S(1)}) custom-call(f32[4,512,512]{2,1,0:T(8,128)S(1)} %copy-done, f32[4,512,512]{2,1,0:T(8,128)S(1)} %copy-done.1, s32[4,512]{1,0:T(4,128)S(1)} %copy-done.2), custom_call_target="tpu_custom_call" | custom-call | flops 4294967296 | bytes 2097152 | tf_op jit(solution)/shard_map/pallas_call | solution.py:210
  28.0 0.0 copy-start.3
  28.0 4.0 %copy-done.3 = bf16[20,512,512]{2,1,0:T(8,128)(2,1)} copy-done((bf16[20,512,512]{2,1,0:T(8,128)(2,1)}, bf16[20,512,512]{2,1,0:T(8,128)(2,1)S(1)}, u32[]{:S(2)}) %copy-start.3) | copy-done | bytes 10485784
  32.0 18.6 %all-to-all-done = f32[256,8,128]{2,1,0:T(8,128)S(1)} async-done(((f32[256,8,128]{2,1,0:T(8,128)}), f32[256,8,128]{2,1,0:T(8,128)S(1)}, u32[]{:S(2)}, u32[]{:S(2)}) %all-to-all-start) | async-done | bytes 1048608 | tf_op jit(solution)/shard_map/all_to_all | solution.py:195
  50.6 7.4 %shard_map.70 = f32[2048,128]{1,0:T(8,128)S(1)} custom-call(f32[2048,128]{1,0:T(8,128)S(1)} %bitcast.5, bf16[4,512,512]{2,1,0:T(8,128)(2,1)S(1)} %get-tuple-element.4.first, bf16[20,512,512]{2,1,0:T(8,128)(2,1)} %copy-done.3), custom_call_target="tpu_custom_call" | custom-call | flops 4831838208 | bytes 2097152 | tf_op jit(solution)/shard_map/pallas_call | solution.py:222
  58.0 38.0 %all_to_all.10 = f32[256,8,128]{2,1,0:T(8,128)S(1)} all-to-all(f32[256,8,128]{2,1,0:T(8,128)S(1)} %bitcast.6), channel_id=1, replica_groups=mesh['outer'=16,'inner'=16] {'inner','outer'}, dimensions={0} | all-to-all | bytes 2097152 | tf_op jit(solution)/shard_map/all_to_all | solution.py:195
  96.0 1.0 %shard_map.71 = (f32[1,1,256,512]{3,2,1,0:T(8,128)}, f32[1,1,256,512]{3,2,1,0:T(8,128)}) custom-call(f32[2048,128]{1,0:T(8,128)S(1)} %bitcast.4), custom_call_target="tpu_custom_call" | custom-call | flops 1000000 | bytes 2097152 | tf_op jit(solution)/shard_map/pallas_call | solution.py:228
Async XLA Ops:
  0.6 17.8 %copy-start.2 = (s32[4,512]{1,0:T(4,128)S(1)}, s32[4,512]{1,0:T(4,128)}, u32[]{:S(2)}) copy-start(s32[4,512]{1,0:T(4,128)} %orders.1) | copy-start | bytes 24580
  2.8 47.8 %all-to-all-start = ((f32[256,8,128]{2,1,0:T(8,128)}), f32[256,8,128]{2,1,0:T(8,128)S(1)}, u32[]{:S(2)}, u32[]{:S(2)}) async-start(f32[256,8,128]{2,1,0:T(8,128)} %bitcast.7), calls=%async_computation | async-start | bytes 2097152 | tf_op jit(solution)/shard_map/all_to_all | solution.py:195
  18.5 2.2 %copy-start = (f32[4,512,512]{2,1,0:T(8,128)S(1)}, f32[4,512,512]{2,1,0:T(8,128)}, u32[]{:S(2)}) copy-start(f32[4,512,512]{2,1,0:T(8,128)} %branch_real.1) | copy-start | bytes 12582916
  20.6 2.2 %copy-start.1 = (f32[4,512,512]{2,1,0:T(8,128)S(1)}, f32[4,512,512]{2,1,0:T(8,128)}, u32[]{:S(2)}) copy-start(f32[4,512,512]{2,1,0:T(8,128)} %branch_imag.1) | copy-start | bytes 12582916
  28.0 4.0 %copy-start.3 = (bf16[20,512,512]{2,1,0:T(8,128)(2,1)}, bf16[20,512,512]{2,1,0:T(8,128)(2,1)S(1)}, u32[]{:S(2)}) copy-start(bf16[20,512,512]{2,1,0:T(8,128)(2,1)S(1)} %get-tuple-element.5.stored) | copy-start | bytes 31457284

commit v4 on v3

--- a/solution.py
+++ b/solution.py
@@ -5,11 +5,13 @@
 from jax import lax
 from jax.experimental import pallas as pl
 from jax.experimental.pallas import tpu as pltpu
+from jax.sharding import Mesh
 from jax.sharding import PartitionSpec as P
 
 PRODUCTS = 4
 LANES = 128
 PARTS = 4
+ORDER = ("zhi", "zlo", "y", "x", "core")
 
 
 def halves(x):
@@ -94,7 +96,11 @@
         leave.wait()
 
 
-def swap_groups(source, target, major):
+def place(inner):
+    return 128 * (inner // 2 % 2) + 2 * (inner // 4) + inner % 2
+
+
+def swap_groups(source, target, first, last):
     lane = lax.broadcasted_iota(jnp.int32, (16, LANES), 1)
     first_half = lane < 64
     even_group = (lane & 32) == 0
@@ -104,7 +110,7 @@
                 v = []
                 for r in range(4):
                     s = 4 * g + r
-                    rows = pl.ds(24 * s, 16) if major else pl.ds(s, 16, stride=24)
+                    rows = pl.ds(place(s), 16, stride=8) if first else pl.ds(s, 16, stride=24)
                     v.append(source[m, q, rows, :])
                 for r in range(2):
                     a, b = v[r], v[r + 2]
@@ -116,12 +122,15 @@
                     v[r] = jnp.where(even_group, a, pltpu.roll(b, 32, 1))
                     v[r + 1] = jnp.where(even_group, pltpu.roll(a, 96, 1), b)
                 for t in range(4):
-                    target[m, g, pl.ds((4 * q + t) * 16, 16), :] = v[t]
+                    s = 4 * q + t
+                    rows = pl.ds(place(s), 16, stride=8) if last else pl.ds(16 * s, 16)
+                    target[m, g, rows, :] = v[t]
 
 
 def multiply(real, imag, tables, left, ready):
+    rows = real.shape[0]
     for k, plane in enumerate((real, imag, real + imag)):
-        left[2 * k], left[2 * k + 1] = halves(plane)
+        left[k, :rows], left[k, rows:] = halves(plane)
     width = real.shape[1]
     step = 256
     for n in range(width // step):
@@ -130,9 +139,9 @@
         for k in range(3):
             if n == 0:
                 ready(k)
-            high, low = left[2 * k], left[2 * k + 1]
             right_h, right_l = (table[place, :, columns] for table, place in tables[2 * k:2 * k + 2])
-            terms.append(dot(high, right_h) + dot(low, right_h) + dot(high, right_l))
+            both = dot(left[k], right_h)
+            terms.append(both[:rows] + both[rows:] + dot(left[k, :rows], right_l))
         out_real, out_imag = terms[0] - terms[1], terms[2] - terms[0] - terms[1]
         for j in range(step // LANES):
             tile = slice(j * LANES, (j + 1) * LANES)
@@ -154,7 +163,7 @@
                 for m in range(2)
             )
         else:
-            swap_groups(work, turned, p == 1)
+            swap_groups(work, turned, p == 1, p == PRODUCTS - 1)
             real, imag = (jnp.concatenate([turned[m, q] for q in range(4)], axis=1) for m in range(2))
         tables = [(later, span.start + j) for j in range(span.size)]
         if p == 0:
@@ -165,7 +174,10 @@
                 fetches[p].wait()
 
         for q, out_real, out_imag in multiply(real, imag, tables, left, ready):
-            if p < PRODUCTS - 1:
+            if p == 0:
+                work[0, q, :rows] = out_real
+                work[1, q, :rows] = out_imag
+            elif p < PRODUCTS - 1:
                 for u in range(16):
                     work[0, q, 24 * u:24 * u + 16] = out_real[16 * u:16 * u + 16]
                     work[1, q, 24 * u:24 * u + 16] = out_imag[16 * u:16 * u + 16]
@@ -192,7 +204,7 @@
 
 def exchange(packed):
     pieces = packed.reshape(-1, 8, LANES)
-    pieces = lax.all_to_all(pieces, ("inner", "outer"), split_axis=0, concat_axis=0, tiled=True)
+    pieces = lax.all_to_all(pieces, ORDER, split_axis=0, concat_axis=0, tiled=True)
     return pieces.reshape(packed.shape)
 
 
@@ -215,7 +227,7 @@
         pltpu.VMEM((2, 4, 384, LANES), jnp.float32),
         tiled,
         pltpu.VMEM(stored.shape, stored.dtype),
-        pltpu.VMEM((6, rows, width), stored.dtype),
+        pltpu.VMEM((3, 2 * rows, width), stored.dtype),
         dma((PRODUCTS,)),
     ]
     flops = 2 * 36 * rows * width**2
@@ -230,11 +242,12 @@
 
 
 def solution(mesh):
-    placed = (P("outer", "inner", None, None), P("outer", "inner", None, None), P(), P(), P())
+    chips = Mesh(mesh.devices.reshape(4, 4, 4, 2, 2), ("zlo", "y", "x", "zhi", "core"))
+    stem = P(("zlo", "y"), ("x", "zhi", "core"), None, None)
     return jax.shard_map(
         on_device,
-        mesh=mesh,
-        in_specs=placed,
-        out_specs=(P("outer", "inner", None, None), P("outer", "inner", None, None)),
+        mesh=chips,
+        in_specs=(stem, stem, P(), P(), P()),
+        out_specs=(stem, stem),
         check_vma=False,
     )

time: 97.3 us -> 94.7 us (0.973)
  waiting for transfers between devices: 18.6 us -> 17.1 us
  blocking collectives: 38 us -> 36.8 us
    all_to_all x1, waiting for transfers between devices: 18.6 us -> 17.1 us  [exchange(): lax.all_to_all(pieces, ORDER, split_axis=0, concat_axis=0, tiled=True)]
    all_to_all x1, blocking collectives: 38 us -> 36.8 us  [exchange(): lax.all_to_all(pieces, ORDER, split_axis=0, concat_axis=0, tiled=True)]
where the time goes in v4:
time: 94.7 us; the launch traced here: 94.5 us
  blocking collectives  36.8 us (39%)
  waiting for transfers between devices  17.1 us (18%)
  Pallas kernels  15.9 us (17%)
  starting transfers between devices  15.7 us (17%)
  local copies, waits for them, and re-layouts  8.34 us (9%)
    all_to_all x1, blocking collectives, exchange(): lax.all_to_all(pieces, ORDER, split_axis=0, concat_axis=0, tiled=True)  36.8 us
    all_to_all x1, waiting for transfers between devices, exchange(): lax.all_to_all(pieces, ORDER, split_axis=0, concat_axis=0, tiled=True)  17.1 us
    all_to_all x1, starting transfers between devices, exchange(): lax.all_to_all(pieces, ORDER, split_axis=0, concat_axis=0, tiled=True)  15.7 us
    unnamed x8, local copies, waits for them, and re-layouts  8.34 us
    pallas_call x1, Pallas kernels, on_device(): call(stages_kernel, packed, [VMEM, VMEM, HBM], VMEM, flops, scratch, 40 *...  7.6 us
    pallas_call x1, Pallas kernels, on_device(): call(tables_kernel, (first, stored), [VMEM] * 3, (VMEM, VMEM), 32 * width...  5.14 us
    pallas_call x1, Pallas kernels, on_device(): call(pack_kernel, packed, [HBM] * 2, HBM, 10 ** 6, scratch)  2.13 us
  transfers between devices with their start and end apart: 1, of which 1 were waited for; matrix products, arithmetic and copies ran while one was open for 0% of the time, Pallas kernels for 5%

profile of v4, /device:TPU:1, one launch (start us, length us, event | category | flops | bytes accessed | tf_op | source)
XLA Modules:
  0.0 94.5 jit_solution(8420561095102304000)
XLA Ops:
  0.6 0.0 copy-start.2
  0.6 2.1 %shard_map.68 = f32[2048,128]{1,0:T(8,128)} custom-call(f32[1,1,256,512]{3,2,1,0:T(8,128)} %plane_real.1, f32[1,1,256,512]{3,2,1,0:T(8,128)} %plane_imag.1), custom_call_target="tpu_custom_call" | custom-call | flops 1000000 | bytes 2097152 | tf_op jit(solution)/shard_map/pallas_call | solution.py:219
  2.8 15.7 %all-to-all-start = ((f32[256,8,128]{2,1,0:T(8,128)}), f32[256,8,128]{2,1,0:T(8,128)S(1)}, u32[]{:S(2)}, u32[]{:S(2)}) async-start(f32[256,8,128]{2,1,0:T(8,128)} %bitcast.7), calls=%async_computation | async-start | bytes 2097152 | tf_op jit(solution)/shard_map/all_to_all | solution.py:207
  18.4 0.0 copy-done.2
  18.5 0.0 copy-start
  18.5 2.2 %copy-done = f32[4,512,512]{2,1,0:T(8,128)S(1)} copy-done((f32[4,512,512]{2,1,0:T(8,128)S(1)}, f32[4,512,512]{2,1,0:T(8,128)}, u32[]{:S(2)}) %copy-start) | copy-done | bytes 4194328
  20.6 0.0 copy-start.1
  20.6 2.2 %copy-done.1 = f32[4,512,512]{2,1,0:T(8,128)S(1)} copy-done((f32[4,512,512]{2,1,0:T(8,128)S(1)}, f32[4,512,512]{2,1,0:T(8,128)}, u32[]{:S(2)}) %copy-start.1) | copy-done | bytes 4194328
  22.8 5.1 %shard_map.69 = (bf16[4,512,512]{2,1,0:T(8,128)(2,1)S(1)}, bf16[20,512,512]{2,1,0:T(8,128)(2,1)S(1)}) custom-call(f32[4,512,512]{2,1,0:T(8,128)S(1)} %copy-done, f32[4,512,512]{2,1,0:T(8,128)S(1)} %copy-done.1, s32[4,512]{1,0:T(4,128)S(1)} %copy-done.2), custom_call_target="tpu_custom_call" | custom-call | flops 4294967296 | bytes 2097152 | tf_op jit(solution)/shard_map/pallas_call | solution.py:222
  28.0 0.0 copy-start.3
  28.0 4.0 %copy-done.3 = bf16[20,512,512]{2,1,0:T(8,128)(2,1)} copy-done((bf16[20,512,512]{2,1,0:T(8,128)(2,1)}, bf16[20,512,512]{2,1,0:T(8,128)(2,1)S(1)}, u32[]{:S(2)}) %copy-start.3) | copy-done | bytes 10485784
  32.0 17.1 %all-to-all-done = f32[256,8,128]{2,1,0:T(8,128)S(1)} async-done(((f32[256,8,128]{2,1,0:T(8,128)}), f32[256,8,128]{2,1,0:T(8,128)S(1)}, u32[]{:S(2)}, u32[]{:S(2)}) %all-to-all-start) | async-done | bytes 1048608 | tf_op jit(solution)/shard_map/all_to_all | solution.py:207
  49.0 7.6 %shard_map.70 = f32[2048,128]{1,0:T(8,128)S(1)} custom-call(f32[2048,128]{1,0:T(8,128)S(1)} %bitcast.5, bf16[4,512,512]{2,1,0:T(8,128)(2,1)S(1)} %get-tuple-element.4.first, bf16[20,512,512]{2,1,0:T(8,128)(2,1)} %copy-done.3), custom_call_target="tpu_custom_call" | custom-call | flops 4831838208 | bytes 2097152 | tf_op jit(solution)/shard_map/pallas_call | solution.py:234
  56.6 36.8 %all_to_all.10 = f32[256,8,128]{2,1,0:T(8,128)S(1)} all-to-all(f32[256,8,128]{2,1,0:T(8,128)S(1)} %bitcast.6), channel_id=1, replica_groups=mesh['zlo'=4,'y'=4,'x'=4,'zhi'=2,'core'=2] {'zhi','zlo','y','x','core'}, dimensions={0} | all-to-all | bytes 2097152 | tf_op jit(solution)/shard_map/all_to_all | solution.py:207
  93.4 1.0 %shard_map.71 = (f32[1,1,256,512]{3,2,1,0:T(8,128)}, f32[1,1,256,512]{3,2,1,0:T(8,128)}) custom-call(f32[2048,128]{1,0:T(8,128)S(1)} %bitcast.4), custom_call_target="tpu_custom_call" | custom-call | flops 1000000 | bytes 2097152 | tf_op jit(solution)/shard_map/pallas_call | solution.py:240
Async XLA Ops:
  0.6 17.8 %copy-start.2 = (s32[4,512]{1,0:T(4,128)S(1)}, s32[4,512]{1,0:T(4,128)}, u32[]{:S(2)}) copy-start(s32[4,512]{1,0:T(4,128)} %orders.1) | copy-start | bytes 24580
  2.8 46.2 %all-to-all-start = ((f32[256,8,128]{2,1,0:T(8,128)}), f32[256,8,128]{2,1,0:T(8,128)S(1)}, u32[]{:S(2)}, u32[]{:S(2)}) async-start(f32[256,8,128]{2,1,0:T(8,128)} %bitcast.7), calls=%async_computation | async-start | bytes 2097152 | tf_op jit(solution)/shard_map/all_to_all | solution.py:207
  18.5 2.2 %copy-start = (f32[4,512,512]{2,1,0:T(8,128)S(1)}, f32[4,512,512]{2,1,0:T(8,128)}, u32[]{:S(2)}) copy-start(f32[4,512,512]{2,1,0:T(8,128)} %branch_real.1) | copy-start | bytes 12582916
  20.6 2.2 %copy-start.1 = (f32[4,512,512]{2,1,0:T(8,128)S(1)}, f32[4,512,512]{2,1,0:T(8,128)}, u32[]{:S(2)}) copy-start(f32[4,512,512]{2,1,0:T(8,128)} %branch_imag.1) | copy-start | bytes 12582916
  28.0 4.0 %copy-start.3 = (bf16[20,512,512]{2,1,0:T(8,128)(2,1)}, bf16[20,512,512]{2,1,0:T(8,128)(2,1)S(1)}, u32[]{:S(2)}) copy-start(bf16[20,512,512]{2,1,0:T(8,128)(2,1)S(1)} %get-tuple-element.5.stored) | copy-start | bytes 31457284

commit v5 on v4

--- a/solution.py
+++ b/solution.py
@@ -24,7 +24,7 @@
 
 
 def spans():
-    counts = [2] + [6] * (PRODUCTS - 1)
+    counts = [0] + [4] * (PRODUCTS - 1)
     return [pl.ds(sum(counts[:p]), count) for p, count in enumerate(counts)]
 
 
@@ -33,18 +33,12 @@
     places = lax.broadcasted_iota(jnp.int32, (width, width), 0)
     for p, span in enumerate(spans()):
         selector = (places == orders[p, :][None, :]).astype(jnp.float32).astype(jnp.bfloat16)
-        last = span.start + span.size
-        moved = []
         for m, plane in enumerate((branch_real, branch_imag)):
             high, low = halves(plane[p])
             high, low = dot(selector, high), dot(selector, low)
             table, place = (first, 2 * m) if p == 0 else (stored, span.start + 2 * m)
             table[place] = high.astype(jnp.bfloat16)
             table[place + 1] = low.astype(jnp.bfloat16)
-            moved.append(high + low)
-        high, low = halves(moved[0] + moved[1])
-        stored[last - 2] = high
-        stored[last - 1] = low
 
 
 def pack_kernel(plane_real, plane_imag, packed, planes, tiles, arrived, left):
@@ -148,13 +142,13 @@
             yield n * (step // LANES) + j, out_real[:, tile], out_imag[:, tile]
 
 
-def stages_kernel(received, first, stored, sent, work, turned, later, left, arrived):
+def stages_kernel(received, first, stored, sent, work, turned, later, left, sums, arrived):
     rows = received.shape[0] // 8
     fetches = [
-        pltpu.make_async_copy(stored.at[span], later.at[span], arrived.at[p]) for p, span in enumerate(spans())
+        pltpu.make_async_copy(stored.at[span], later.at[span], arrived.at[p - 1]) for p, span in enumerate(spans()) if p > 0
     ]
-    for p, fetch in enumerate(fetches):
-        fetch.start(priority=min(p, 1))
+    for fetch in fetches:
+        fetch.start()
 
     for p, span in enumerate(spans()):
         if p == 0:
@@ -167,11 +161,16 @@
             real, imag = (jnp.concatenate([turned[m, q] for q in range(4)], axis=1) for m in range(2))
         tables = [(later, span.start + j) for j in range(span.size)]
         if p == 0:
-            tables = [(first, j) for j in range(4)] + tables
-
-        def ready(k, p=p):
-            if k == (2 if p == 0 else 0):
-                fetches[p].wait()
+            tables = [(first, j) for j in range(4)]
+        if len(tables) == 4:
+            tables += [(sums, 0), (sums, 1)]
+
+        def ready(k, p=p, tables=tables):
+            if k == 0 and p > 0:
+                fetches[p - 1].wait()
+            if k == 1 and tables[4][0] is sums:
+                parts = [table[place].astype(jnp.float32) for table, place in tables[:4]]
+                sums[0], sums[1] = halves((parts[0] + parts[1]) + (parts[2] + parts[3]))
 
         for q, out_real, out_imag in multiply(real, imag, tables, left, ready):
             if p == 0:
@@ -218,7 +217,7 @@
     scratch = [planes, pltpu.VMEM(packed.shape, packed.dtype), dma((2, PARTS)), dma((PARTS,))]
     sent = call(pack_kernel, packed, [HBM] * 2, HBM, 10**6, scratch)(stem_real, stem_imag)
     first = jax.ShapeDtypeStruct((4, width, width), jnp.bfloat16)
-    stored = jax.ShapeDtypeStruct((6 * PRODUCTS - 4, width, width), jnp.bfloat16)
+    stored = jax.ShapeDtypeStruct((4 * PRODUCTS - 4, width, width), jnp.bfloat16)
     first, stored = call(
         tables_kernel, (first, stored), [VMEM] * 3, (VMEM, VMEM), 32 * width**3, (), 32 * 2**20
     )(branch_real, branch_imag, orders)
@@ -228,7 +227,8 @@
         tiled,
         pltpu.VMEM(stored.shape, stored.dtype),
         pltpu.VMEM((3, 2 * rows, width), stored.dtype),
-        dma((PRODUCTS,)),
+        pltpu.VMEM((2, width, width), stored.dtype),
+        dma((PRODUCTS - 1,)),
     ]
     flops = 2 * 36 * rows * width**2
     sent = call(stages_kernel, packed, [VMEM, VMEM, HBM], VMEM, flops, scratch, 40 * 2**20)(

time: 94.7 us -> 97.3 us (1.027)
  waiting for transfers between devices: 17.1 us -> 18.9 us
  local copies, waits for them, and re-layouts: 8.34 us -> 9.81 us
    all_to_all x1, waiting for transfers between devices: 17.1 us -> 18.9 us  [exchange(): lax.all_to_all(pieces, ORDER, split_axis=0, concat_axis=0, tiled=True)]
    unnamed x8 -> x10, local copies, waits for them, and re-layouts: 8.34 us -> 9.81 us
where the time goes in v5:
time: 97.3 us; the launch traced here: 97 us
  blocking collectives  36.8 us (38%)
  waiting for transfers between devices  18.9 us (19%)
  starting transfers between devices  15.7 us (16%)
  Pallas kernels  15.1 us (16%)
  local copies, waits for them, and re-layouts  9.81 us (10%)
    all_to_all x1, blocking collectives, exchange(): lax.all_to_all(pieces, ORDER, split_axis=0, concat_axis=0, tiled=True)  36.8 us
    all_to_all x1, waiting for transfers between devices, exchange(): lax.all_to_all(pieces, ORDER, split_axis=0, concat_axis=0, tiled=True)  18.9 us
    all_to_all x1, starting transfers between devices, exchange(): lax.all_to_all(pieces, ORDER, split_axis=0, concat_axis=0, tiled=True)  15.7 us
    unnamed x10, local copies, waits for them, and re-layouts  9.81 us
    pallas_call x1, Pallas kernels, on_device(): call(stages_kernel, packed, [VMEM, VMEM, HBM], VMEM, flops, scratch, 40 *...  7.36 us
    pallas_call x1, Pallas kernels, on_device(): call(tables_kernel, (first, stored), [VMEM] * 3, (VMEM, VMEM), 32 * width...  4.56 us
    pallas_call x1, Pallas kernels, on_device(): call(pack_kernel, packed, [HBM] * 2, HBM, 10 ** 6, scratch)  2.14 us
  transfers between devices with their start and end apart: 1, of which 1 were waited for; matrix products, arithmetic and copies ran while one was open for 0% of the time, Pallas kernels for 5%

profile of v5, /device:TPU:1, one launch (start us, length us, event | category | flops | bytes accessed | tf_op | source)
XLA Modules:
  0.0 97.0 jit_solution(18255053471783499503)
XLA Ops:
  0.6 0.0 copy-start.2
  0.6 2.1 %shard_map.68 = f32[2048,128]{1,0:T(8,128)} custom-call(f32[1,1,256,512]{3,2,1,0:T(8,128)} %plane_real.1, f32[1,1,256,512]{3,2,1,0:T(8,128)} %plane_imag.1), custom_call_target="tpu_custom_call" | custom-call | flops 1000000 | bytes 2097152 | tf_op jit(solution)/shard_map/pallas_call | solution.py:218
  2.8 15.7 %all-to-all-start = ((f32[256,8,128]{2,1,0:T(8,128)}), f32[256,8,128]{2,1,0:T(8,128)S(1)}, u32[]{:S(2)}, u32[]{:S(2)}) async-start(f32[256,8,128]{2,1,0:T(8,128)} %bitcast.7), calls=%async_computation | async-start | bytes 2097152 | tf_op jit(solution)/shard_map/all_to_all | solution.py:206
  18.4 0.0 copy-done.2
  18.5 0.0 copy-start
  18.5 2.2 %copy-done = f32[4,512,512]{2,1,0:T(8,128)S(1)} copy-done((f32[4,512,512]{2,1,0:T(8,128)S(1)}, f32[4,512,512]{2,1,0:T(8,128)}, u32[]{:S(2)}) %copy-start) | copy-done | bytes 4194328
  20.6 0.0 copy-start.1
  20.6 2.2 %copy-done.1 = f32[4,512,512]{2,1,0:T(8,128)S(1)} copy-done((f32[4,512,512]{2,1,0:T(8,128)S(1)}, f32[4,512,512]{2,1,0:T(8,128)}, u32[]{:S(2)}) %copy-start.1) | copy-done | bytes 4194328
  22.8 4.6 %shard_map.69 = (bf16[4,512,512]{2,1,0:T(8,128)(2,1)S(1)}, bf16[12,512,512]{2,1,0:T(8,128)(2,1)S(1)}) custom-call(f32[4,512,512]{2,1,0:T(8,128)S(1)} %copy-done, f32[4,512,512]{2,1,0:T(8,128)S(1)} %copy-done.1, s32[4,512]{1,0:T(4,128)S(1)} %copy-done.2), custom_call_target="tpu_custom_call" | custom-call | flops 4294967296 | bytes 2097152 | tf_op jit(solution)/shard_map/pallas_call | solution.py:221
  27.4 0.0 copy-start.3
  27.4 2.6 %copy-done.3 = bf16[12,512,512]{2,1,0:T(8,128)(2,1)} copy-done((bf16[12,512,512]{2,1,0:T(8,128)(2,1)}, bf16[12,512,512]{2,1,0:T(8,128)(2,1)S(1)}, u32[]{:S(2)}) %copy-start.3) | copy-done | bytes 6291480
  30.1 18.9 %all-to-all-done = f32[256,8,128]{2,1,0:T(8,128)S(1)} async-done(((f32[256,8,128]{2,1,0:T(8,128)}), f32[256,8,128]{2,1,0:T(8,128)S(1)}, u32[]{:S(2)}, u32[]{:S(2)}) %all-to-all-start) | async-done | bytes 1048608 | tf_op jit(solution)/shard_map/all_to_all | solution.py:206
  49.0 0.0 copy-start.4
  49.0 2.8 %copy-done.4 = bf16[12,512,512]{2,1,0:T(8,128)(2,1)S(1)} copy-done((bf16[12,512,512]{2,1,0:T(8,128)(2,1)S(1)}, bf16[12,512,512]{2,1,0:T(8,128)(2,1)}, u32[]{:S(2)}) %copy-start.4) | copy-done | bytes 6291480
  51.8 7.4 %shard_map.70 = f32[2048,128]{1,0:T(8,128)S(1)} custom-call(f32[2048,128]{1,0:T(8,128)S(1)} %bitcast.5, bf16[4,512,512]{2,1,0:T(8,128)(2,1)S(1)} %get-tuple-element.4.first, bf16[12,512,512]{2,1,0:T(8,128)(2,1)S(1)} %copy-done.4), custom_call_target="tpu_custom_call" | custom-call | flops 4831838208 | bytes 2097152 | tf_op jit(solution)/shard_map/pallas_call | solution.py:234
  59.2 36.8 %all_to_all.10 = f32[256,8,128]{2,1,0:T(8,128)S(1)} all-to-all(f32[256,8,128]{2,1,0:T(8,128)S(1)} %bitcast.6), channel_id=1, replica_groups=mesh['zlo'=4,'y'=4,'x'=4,'zhi'=2,'core'=2] {'zhi','zlo','y','x','core'}, dimensions={0} | all-to-all | bytes 2097152 | tf_op jit(solution)/shard_map/all_to_all | solution.py:206
  96.0 1.0 %shard_map.71 = (f32[1,1,256,512]{3,2,1,0:T(8,128)}, f32[1,1,256,512]{3,2,1,0:T(8,128)}) custom-call(f32[2048,128]{1,0:T(8,128)S(1)} %bitcast.4), custom_call_target="tpu_custom_call" | custom-call | flops 1000000 | bytes 2097152 | tf_op jit(solution)/shard_map/pallas_call | solution.py:240
Async XLA Ops:
  0.6 17.8 %copy-start.2 = (s32[4,512]{1,0:T(4,128)S(1)}, s32[4,512]{1,0:T(4,128)}, u32[]{:S(2)}) copy-start(s32[4,512]{1,0:T(4,128)} %orders.1) | copy-start | bytes 24580
  2.8 46.2 %all-to-all-start = ((f32[256,8,128]{2,1,0:T(8,128)}), f32[256,8,128]{2,1,0:T(8,128)S(1)}, u32[]{:S(2)}, u32[]{:S(2)}) async-start(f32[256,8,128]{2,1,0:T(8,128)} %bitcast.7), calls=%async_computation | async-start | bytes 2097152 | tf_op jit(solution)/shard_map/all_to_all | solution.py:206
  18.5 2.2 %copy-start = (f32[4,512,512]{2,1,0:T(8,128)S(1)}, f32[4,512,512]{2,1,0:T(8,128)}, u32[]{:S(2)}) copy-start(f32[4,512,512]{2,1,0:T(8,128)} %branch_real.1) | copy-start | bytes 12582916
  20.6 2.2 %copy-start.1 = (f32[4,512,512]{2,1,0:T(8,128)S(1)}, f32[4,512,512]{2,1,0:T(8,128)}, u32[]{:S(2)}) copy-start(f32[4,512,512]{2,1,0:T(8,128)} %branch_imag.1) | copy-start | bytes 12582916
  27.4 2.7 %copy-start.3 = (bf16[12,512,512]{2,1,0:T(8,128)(2,1)}, bf16[12,512,512]{2,1,0:T(8,128)(2,1)S(1)}, u32[]{:S(2)}) copy-start(bf16[12,512,512]{2,1,0:T(8,128)(2,1)S(1)} %get-tuple-element.5.stored) | copy-start | bytes 18874372
  49.0 2.8 %copy-start.4 = (bf16[12,512,512]{2,1,0:T(8,128)(2,1)S(1)}, bf16[12,512,512]{2,1,0:T(8,128)(2,1)}, u32[]{:S(2)}) copy-start(bf16[12,512,512]{2,1,0:T(8,128)(2,1)} %copy-done.3) | copy-start | bytes 18874372

commit v6 on v4

--- a/solution.py
+++ b/solution.py
@@ -11,7 +11,7 @@
 PRODUCTS = 4
 LANES = 128
 PARTS = 4
-ORDER = ("zhi", "zlo", "y", "x", "core")
+ORDER = ("x", "zhi", "zlo", "y", "core")
 
 
 def halves(x):
@@ -97,7 +97,7 @@
 
 
 def place(inner):
-    return 128 * (inner // 2 % 2) + 2 * (inner // 4) + inner % 2
+    return 64 * (inner // 4) + 32 * (inner // 2 % 2) + inner % 2
 
 
 def swap_groups(source, target, first, last):
@@ -110,7 +110,7 @@
                 v = []
                 for r in range(4):
                     s = 4 * g + r
-                    rows = pl.ds(place(s), 16, stride=8) if first else pl.ds(s, 16, stride=24)
+                    rows = pl.ds(place(s), 16, stride=2) if first else pl.ds(s, 16, stride=24)
                     v.append(source[m, q, rows, :])
                 for r in range(2):
                     a, b = v[r], v[r + 2]
@@ -123,7 +123,7 @@
                     v[r + 1] = jnp.where(even_group, pltpu.roll(a, 96, 1), b)
                 for t in range(4):
                     s = 4 * q + t
-                    rows = pl.ds(place(s), 16, stride=8) if last else pl.ds(16 * s, 16)
+                    rows = pl.ds(place(s), 16, stride=2) if last else pl.ds(16 * s, 16)
                     target[m, g, rows, :] = v[t]
 
 

time: 94.7 us -> 95.4 us (level)
  no operation moved by 1% of the time
where the time goes in v6:
time: 95.4 us; the launch traced here: 95.2 us
  blocking collectives  37.2 us (39%)
  waiting for transfers between devices  17.4 us (18%)
  Pallas kernels  15.9 us (17%)
  starting transfers between devices  15.7 us (16%)
  local copies, waits for them, and re-layouts  8.34 us (9%)
    all_to_all x1, blocking collectives, exchange(): lax.all_to_all(pieces, ORDER, split_axis=0, concat_axis=0, tiled=True)  37.2 us
    all_to_all x1, waiting for transfers between devices, exchange(): lax.all_to_all(pieces, ORDER, split_axis=0, concat_axis=0, tiled=True)  17.4 us
    all_to_all x1, starting transfers between devices, exchange(): lax.all_to_all(pieces, ORDER, split_axis=0, concat_axis=0, tiled=True)  15.7 us
    unnamed x8, local copies, waits for them, and re-layouts  8.34 us
    pallas_call x1, Pallas kernels, on_device(): call(stages_kernel, packed, [VMEM, VMEM, HBM], VMEM, flops, scratch, 40 *...  7.56 us
    pallas_call x1, Pallas kernels, on_device(): call(tables_kernel, (first, stored), [VMEM] * 3, (VMEM, VMEM), 32 * width...  5.14 us
    pallas_call x1, Pallas kernels, on_device(): call(pack_kernel, packed, [HBM] * 2, HBM, 10 ** 6, scratch)  2.13 us
  transfers between devices with their start and end apart: 1, of which 1 were waited for; matrix products, arithmetic and copies ran while one was open for 0% of the time, Pallas kernels for 5%

profile of v6, /device:TPU:1, one launch (start us, length us, event | category | flops | bytes accessed | tf_op | source)
XLA Modules:
  0.0 95.2 jit_solution(2929373675992844710)
XLA Ops:
  0.6 0.0 copy-start.2
  0.6 2.1 %shard_map.68 = f32[2048,128]{1,0:T(8,128)} custom-call(f32[1,1,256,512]{3,2,1,0:T(8,128)} %plane_real.1, f32[1,1,256,512]{3,2,1,0:T(8,128)} %plane_imag.1), custom_call_target="tpu_custom_call" | custom-call | flops 1000000 | bytes 2097152 | tf_op jit(solution)/shard_map/pallas_call | solution.py:219
  2.8 15.7 %all-to-all-start = ((f32[256,8,128]{2,1,0:T(8,128)}), f32[256,8,128]{2,1,0:T(8,128)S(1)}, u32[]{:S(2)}, u32[]{:S(2)}) async-start(f32[256,8,128]{2,1,0:T(8,128)} %bitcast.7), calls=%async_computation | async-start | bytes 2097152 | tf_op jit(solution)/shard_map/all_to_all | solution.py:207
  18.4 0.0 copy-done.2
  18.5 0.0 copy-start
  18.5 2.2 %copy-done = f32[4,512,512]{2,1,0:T(8,128)S(1)} copy-done((f32[4,512,512]{2,1,0:T(8,128)S(1)}, f32[4,512,512]{2,1,0:T(8,128)}, u32[]{:S(2)}) %copy-start) | copy-done | bytes 4194328
  20.6 0.0 copy-start.1
  20.6 2.2 %copy-done.1 = f32[4,512,512]{2,1,0:T(8,128)S(1)} copy-done((f32[4,512,512]{2,1,0:T(8,128)S(1)}, f32[4,512,512]{2,1,0:T(8,128)}, u32[]{:S(2)}) %copy-start.1) | copy-done | bytes 4194328
  22.8 5.1 %shard_map.69 = (bf16[4,512,512]{2,1,0:T(8,128)(2,1)S(1)}, bf16[20,512,512]{2,1,0:T(8,128)(2,1)S(1)}) custom-call(f32[4,512,512]{2,1,0:T(8,128)S(1)} %copy-done, f32[4,512,512]{2,1,0:T(8,128)S(1)} %copy-done.1, s32[4,512]{1,0:T(4,128)S(1)} %copy-done.2), custom_call_target="tpu_custom_call" | custom-call | flops 4294967296 | bytes 2097152 | tf_op jit(solution)/shard_map/pallas_call | solution.py:222
  28.0 0.0 copy-start.3
  28.0 4.0 %copy-done.3 = bf16[20,512,512]{2,1,0:T(8,128)(2,1)} copy-done((bf16[20,512,512]{2,1,0:T(8,128)(2,1)}, bf16[20,512,512]{2,1,0:T(8,128)(2,1)S(1)}, u32[]{:S(2)}) %copy-start.3) | copy-done | bytes 10485784
  32.0 17.4 %all-to-all-done = f32[256,8,128]{2,1,0:T(8,128)S(1)} async-done(((f32[256,8,128]{2,1,0:T(8,128)}), f32[256,8,128]{2,1,0:T(8,128)S(1)}, u32[]{:S(2)}, u32[]{:S(2)}) %all-to-all-start) | async-done | bytes 1048608 | tf_op jit(solution)/shard_map/all_to_all | solution.py:207
  49.4 7.6 %shard_map.70 = f32[2048,128]{1,0:T(8,128)S(1)} custom-call(f32[2048,128]{1,0:T(8,128)S(1)} %bitcast.5, bf16[4,512,512]{2,1,0:T(8,128)(2,1)S(1)} %get-tuple-element.4.first, bf16[20,512,512]{2,1,0:T(8,128)(2,1)} %copy-done.3), custom_call_target="tpu_custom_call" | custom-call | flops 4831838208 | bytes 2097152 | tf_op jit(solution)/shard_map/pallas_call | solution.py:234
  57.0 37.2 %all_to_all.10 = f32[256,8,128]{2,1,0:T(8,128)S(1)} all-to-all(f32[256,8,128]{2,1,0:T(8,128)S(1)} %bitcast.6), channel_id=1, replica_groups=mesh['zlo'=4,'y'=4,'x'=4,'zhi'=2,'core'=2] {'x','zhi','zlo','y','core'}, dimensions={0} | all-to-all | bytes 2097152 | tf_op jit(solution)/shard_map/all_to_all | solution.py:207
  94.1 1.0 %shard_map.71 = (f32[1,1,256,512]{3,2,1,0:T(8,128)}, f32[1,1,256,512]{3,2,1,0:T(8,128)}) custom-call(f32[2048,128]{1,0:T(8,128)S(1)} %bitcast.4), custom_call_target="tpu_custom_call" | custom-call | flops 1000000 | bytes 2097152 | tf_op jit(solution)/shard_map/pallas_call | solution.py:240
Async XLA Ops:
  0.6 17.8 %copy-start.2 = (s32[4,512]{1,0:T(4,128)S(1)}, s32[4,512]{1,0:T(4,128)}, u32[]{:S(2)}) copy-start(s32[4,512]{1,0:T(4,128)} %orders.1) | copy-start | bytes 24580
  2.8 46.6 %all-to-all-start = ((f32[256,8,128]{2,1,0:T(8,128)}), f32[256,8,128]{2,1,0:T(8,128)S(1)}, u32[]{:S(2)}, u32[]{:S(2)}) async-start(f32[256,8,128]{2,1,0:T(8,128)} %bitcast.7), calls=%async_computation | async-start | bytes 2097152 | tf_op jit(solution)/shard_map/all_to_all | solution.py:207
  18.5 2.2 %copy-start = (f32[4,512,512]{2,1,0:T(8,128)S(1)}, f32[4,512,512]{2,1,0:T(8,128)}, u32[]{:S(2)}) copy-start(f32[4,512,512]{2,1,0:T(8,128)} %branch_real.1) | copy-start | bytes 12582916
  20.6 2.2 %copy-start.1 = (f32[4,512,512]{2,1,0:T(8,128)S(1)}, f32[4,512,512]{2,1,0:T(8,128)}, u32[]{:S(2)}) copy-start(f32[4,512,512]{2,1,0:T(8,128)} %branch_imag.1) | copy-start | bytes 12582916
  28.0 4.0 %copy-start.3 = (bf16[20,512,512]{2,1,0:T(8,128)(2,1)}, bf16[20,512,512]{2,1,0:T(8,128)(2,1)S(1)}, u32[]{:S(2)}) copy-start(bf16[20,512,512]{2,1,0:T(8,128)(2,1)S(1)} %get-tuple-element.5.stored) | copy-start | bytes 31457284
